TPU v7x, 32 devices: a whole 2x2x4 slice. The times are simulated.
32 devices in a mesh: grp: 2 (over x), ma: 16 (over z, y, core).
Axes of the slice: x: 2, y: 2, z: 4, core: 2. Of those that a mesh axis runs over, the one named last changes fastest.
Arguments:
- tbar_alm: bfloat16 [128, 8, 2, 257], P('ma', 'grp'), parts along dimension 1, may hold values from -6 to 6
- twf_alm: bfloat16 [128, 8, 2, 257], P('ma', 'grp'), parts along dimension 1, may hold values from -6 to 6
- legendre: bfloat16 [128, 257, 16], P('ma'), may hold values from -0.375 to 0.375
- m_slots: int32 [128], replicated, may hold values from 0 to 127, each once
- cycle_order: int32 [16], replicated, may hold values from 0 to 15, each once
- colatitude: float32 [16], replicated, may hold values from 0.35 to 2.79
- cycle_weight: float32 [16], replicated, may hold values from 0.25 to 1
- pixel_mask: int32 [16, 4096], P('ma'), may hold values from 0 to 3
Outputs:
- gradient: float32 [128, 8, 2, 257], P('ma', 'grp'), parts along dimension 1
- curl: float32 [128, 8, 2, 257], P('ma', 'grp'), parts along dimension 1
There are 2 independent parts, one for each index of `grp`. A program takes and returns all parts, laid end to end along the dimension named above; an argument that names none is the same for every part. Nothing has to cross between parts.
Inputs may be any that keep to these rules, and one draw needn't show every extreme that they name: Pair p holds the orders m_slots[p] and 255 - m_slots[p]; each value appears once. Cycle slot i holds cycle cycle_order[i]; each value appears once.
All inputs are finite; a program needn't handle non-finite values.
Results may differ from a plain program's by a relative error of at most 0.017.
Values may be sent and summed in bfloat16 or wider, within the bound.
A program may use at most 128 MiB of HBM per device.

v0:
```python
import math

import functools

import jax
import jax.numpy as jnp
import numpy as np
from jax import lax
from jax.experimental import pallas as pl
from jax.experimental.pallas import tpu as pltpu
from jax.sharding import PartitionSpec as P


def pair_layout(small_orders, mode_count):
    row_index = lax.broadcasted_iota(jnp.int32, (small_orders.shape[0], mode_count + 1), 1)
    smaller = small_orders[:, None]
    upper_half = row_index >= mode_count - smaller
    degree = jnp.where(upper_half, row_index - 1, smaller + row_index)
    orders = jnp.where(upper_half, mode_count - 1 - smaller, smaller + 0 * row_index)
    return (upper_half, degree.astype(jnp.float32), orders.astype(jnp.float32))


def raising(degree, orders):
    square = (
        (degree * degree - orders * orders)
        * (2.0 * degree + 1.0)
        / jnp.maximum(2.0 * degree - 1.0, 1.0)
    )
    return jnp.where(degree > orders, jnp.sqrt(jnp.where(degree > orders, square, 0.0)), 0.0)


def synthesis_sets(tbar_alm, twf_alm, degree, raising_factor, mode_count):
    wiener = twf_alm.astype(jnp.float32)
    scaled = (raising_factor / mode_count)[:, None, None, :] * wiener
    raised = jnp.concatenate([scaled[..., 1:], jnp.zeros_like(scaled[..., :1])], axis=-1)
    stacked = jnp.stack(
        [
            tbar_alm.astype(jnp.float32),
            wiener,
            (degree / mode_count)[:, None, None, :] * wiener,
            raised,
        ],
        axis=2,
    )
    return stacked.reshape(stacked.shape[0], stacked.shape[1], 8, stacked.shape[4]).astype(
        jnp.bfloat16
    )


def mode_columns(small_orders, mode_count):
    return jnp.stack([small_orders, mode_count - 1 - small_orders], axis=1).reshape(-1)


def fourier_table(orders_int, pixel_count):
    pixel_index = lax.broadcasted_iota(jnp.int32, (orders_int.shape[0], pixel_count), 1)
    turns = orders_int[:, None] * pixel_index % pixel_count
    radians = turns.astype(jnp.float32) * (2.0 * math.pi / pixel_count)
    return jnp.stack([jnp.cos(radians), -jnp.sin(radians)], axis=0).astype(jnp.bfloat16)


def combine_modes(legendre_sums, orders_int, cos_cycle, sin_cycle, mode_count):
    orders_real = orders_int.astype(jnp.float32)
    inv_sin = 1.0 / sin_cycle
    ratio = (orders_real / mode_count)[:, None]
    theta_real = (cos_cycle * legendre_sums[:, 4] - legendre_sums[:, 6]) * inv_sin
    theta_imag = (cos_cycle * legendre_sums[:, 5] - legendre_sums[:, 7]) * inv_sin
    phi_real = -ratio * legendre_sums[:, 3] * inv_sin
    phi_imag = ratio * legendre_sums[:, 2] * inv_sin
    weight = (jnp.where(orders_int == 0, 1.0, 2.0) * mode_count ** (-0.5))[:, None]
    stacked = jnp.stack(
        [legendre_sums[:, 0], legendre_sums[:, 1], theta_real, theta_imag, phi_real, phi_imag],
        axis=1,
    )
    return (stacked * weight).astype(jnp.bfloat16)


def analysis_sets(spectra, colatitude, cycle_weight):
    with_cos = cycle_weight * jnp.cos(colatitude) / jnp.sin(colatitude)
    with_sin = cycle_weight / jnp.sin(colatitude)
    stacked = jnp.stack(
        [
            spectra[:, 0] * with_cos,
            spectra[:, 0] * with_sin,
            spectra[:, 1] * with_cos,
            spectra[:, 1] * with_sin,
        ],
        axis=1,
    )
    return stacked.reshape(spectra.shape[0], 8, spectra.shape[3], spectra.shape[4]).astype(
        jnp.bfloat16
    )


def estimate(merged, degree, orders, raising_factor, mode_count, cycle_count):
    level = degree[:, None, :]
    azimuth = orders[:, None, :]
    factor = raising_factor[:, None, :]

    def previous(values):
        return jnp.concatenate([jnp.zeros_like(values[..., :1]), values[..., :-1]], axis=-1)

    grad_real = (
        level * merged[:, :, 0] - factor * previous(merged[:, :, 2]) + azimuth * merged[:, :, 7]
    )
    grad_imag = (
        level * merged[:, :, 1] - factor * previous(merged[:, :, 3]) - azimuth * merged[:, :, 6]
    )
    curl_real = (
        level * merged[:, :, 4] - factor * previous(merged[:, :, 6]) - azimuth * merged[:, :, 3]
    )
    curl_imag = (
        level * merged[:, :, 5] - factor * previous(merged[:, :, 7]) + azimuth * merged[:, :, 2]
    )
    scale = (mode_count / cycle_count) ** 0.5 / jnp.sqrt(jnp.maximum(level * (level + 1.0), 1.0))
    scale = scale[:, :, None, :]
    return (
        jnp.stack([grad_real, grad_imag], axis=2) * scale,
        jnp.stack([curl_real, curl_imag], axis=2) * scale,
    )


def shards(tbar_alm, twf_alm, legendre, m_slots, cycle_order, colatitude, cycle_weight, pixel_mask):
    pairs_dev = tbar_alm.shape[0]
    row_count = tbar_alm.shape[3]
    mode_count = row_count - 1
    cycle_count = legendre.shape[2]
    cycle_dev = pixel_mask.shape[0]
    pixel_count = pixel_mask.shape[1]
    device_slot = lax.axis_index("ma")
    local_small = lax.dynamic_slice_in_dim(m_slots, device_slot * pairs_dev, pairs_dev)
    upper_half, degree, orders = pair_layout(local_small, mode_count)
    raising_factor = raising(degree, orders)
    coeff_sets = synthesis_sets(tbar_alm, twf_alm, degree, raising_factor, mode_count)
    halves = jnp.stack([jnp.logical_not(upper_half), upper_half], axis=1)
    masked = coeff_sets[:, None] * halves.astype(jnp.bfloat16)[:, :, None, None, :]
    legendre_sums = jnp.einsum(
        "phsck,pkr->scphr", masked, legendre, preferred_element_type=jnp.float32
    )
    legendre_sums = jnp.take(legendre_sums, cycle_order, axis=4)
    legendre_sums = legendre_sums.reshape(legendre_sums.shape[0], 8, 2 * pairs_dev, cycle_count)
    all_orders = mode_columns(m_slots, mode_count)
    dft_table = fourier_table(all_orders, pixel_count)
    pixel_weights = pixel_mask.astype(jnp.float32)
    slot_theta = jnp.take(colatitude, cycle_order)
    local_orders = mode_columns(local_small, mode_count)
    outgoing = combine_modes(
        legendre_sums, local_orders, jnp.cos(slot_theta), jnp.sin(slot_theta), mode_count
    )
    fourier = lax.all_to_all(outgoing, "ma", split_axis=3, concat_axis=2, tiled=True)
    fourier = fourier.reshape(fourier.shape[0], 3, 2, mode_count, cycle_dev)
    cycle_maps = jnp.einsum(
        "sqemr,emj->sqrj", fourier, dft_table, preferred_element_type=jnp.float32
    )
    products = (pixel_weights * cycle_maps[:, 0:1] * cycle_maps[:, 1:3]).astype(jnp.bfloat16)
    spectra = jnp.einsum("sqrj,emj->sqemr", products, dft_table, preferred_element_type=jnp.float32)
    received = (spectra * pixel_count ** (-0.5)).astype(jnp.bfloat16)
    returned = lax.all_to_all(received, "ma", split_axis=3, concat_axis=4, tiled=True)
    inverse = (
        jnp.zeros((cycle_count,), jnp.int32).at[cycle_order].set(lax.iota(jnp.int32, cycle_count))
    )
    spectra = jnp.take(returned, inverse, axis=4).astype(jnp.float32)
    weighted = analysis_sets(spectra, colatitude, cycle_weight)
    weighted = weighted.reshape(weighted.shape[0], 8, pairs_dev, 2, cycle_count)
    projected = jnp.einsum(
        "scphr,pkr->phsck", weighted, legendre, preferred_element_type=jnp.float32
    )
    merged = jnp.sum(projected * halves.astype(jnp.float32)[:, :, None, None, :], axis=1)
    return estimate(merged, degree, orders, raising_factor, mode_count, cycle_count)


LANES = 128
F32 = jnp.float32
BF16 = jnp.bfloat16


def split_tables(mode_count, pixel_count, sims):
    m = np.arange(mode_count)[None, :]
    low = np.arange(LANES)[:, None]
    high = np.repeat(np.arange(pixel_count // LANES), sims)[:, None] * LANES
    fine = (m * low % pixel_count) * (2.0 * math.pi / pixel_count)
    coarse = (m * high % pixel_count) * (2.0 * math.pi / pixel_count)
    cos_high = np.cos(coarse).astype(np.float32)
    sin_high = np.sin(coarse).astype(np.float32)

    def halves(values):
        upper = values.astype(BF16)
        return upper, (values - upper.astype(np.float32)).astype(BF16)

    return np.concatenate(
        [np.cos(fine).astype(BF16), (-np.sin(fine)).astype(BF16)]
        + list(halves(cos_high))
        + list(halves(sin_high)),
        axis=0,
    )


def iota(shape, axis):
    return lax.broadcasted_iota(jnp.int32, shape, axis)


def div(values, size):
    return values >> (size.bit_length() - 1)


def mod(values, size):
    return values & (size - 1)


def one_hot(condition):
    return jnp.where(condition, 1.0, 0.0).astype(BF16)


def dot(left, right):
    return jnp.dot(left, right, preferred_element_type=F32)


def dot_t(left, right):
    return lax.dot_general(left, right, (((1,), (1,)), ((), ())), preferred_element_type=F32)


def fused_kernel(
    n, modes, rows, cycles, pixels, sims,
    slots_s, cycle_s, colat_s, weight_s, slots_v, tbar_hbm, twf_hbm, leg_hbm, mask_hbm,
    table_hbm, grad_ref, curl_ref, tbar_ref, twf_ref, leg_ref, mask_ref, table_v, leg_all, prev_all, send_f, recv_f, send_p, recv_p,
    load_sem, fs_sem, fr_sem, ps_sem, pr_sem,
):
    me = lax.axis_index("ma")
    pairs, padded = tbar_ref.shape[0], rows
    block = 2 * pairs
    comps = 2 * sims
    span = 2 * cycles
    total = pairs * span
    barrier = pltpu.get_barrier_semaphore()
    for off in range(1, n):
        pl.semaphore_signal(
            barrier, inc=1, device_id={"ma": lax.rem(me + off, n)},
            device_id_type=pl.DeviceIdType.MESH,
        )

    loads = [
        pltpu.make_async_copy(source, target, load_sem.at[at])
        for at, (source, target) in enumerate(
            [(leg_hbm, leg_ref), (tbar_hbm, tbar_ref), (twf_hbm, twf_ref),
             (table_hbm, table_v), (mask_hbm, mask_ref)]
        )
    ]
    for load in loads:
        load.start()

    row_shape = (pairs, padded)
    smaller = jnp.zeros(row_shape, jnp.int32)
    for p in range(pairs):
        smaller = jnp.where(iota(row_shape, 0) == p, slots_s[me * pairs + p], smaller)
    k = iota(row_shape, 1)
    upper = k >= modes - smaller
    degree = jnp.where(upper, k - 1, smaller + k).astype(F32)
    orders = jnp.where(upper, modes - 1 - smaller, smaller).astype(F32)
    eps = raising(degree, orders)
    upper_f = jnp.where(upper, 1.0, 0.0)
    lower_f = 1.0 - upper_f

    colat = jnp.zeros((cycles, 4 * comps), F32)
    for r in range(cycles):
        colat = jnp.where(iota(colat.shape, 0) == r, colat_s[r], colat)
    csc = 1.0 / jnp.sin(colat)
    cot = jnp.cos(colat) * csc
    lane = iota(colat.shape, 1)
    group = div(lane, comps)
    part_a = jnp.where(group == 0, 1.0, jnp.where(group == 1, cot, 0.0))
    part_m = jnp.where(group == 2, csc, 0.0)
    part_b = jnp.where(group == 1, csc, 0.0)

    blank = jnp.zeros((comps, padded), F32)
    pieces = []
    for load in loads[:3]:
        load.wait()
    for p in range(pairs):
        tbar = jnp.concatenate([tbar_ref[p, s].astype(F32) for s in range(sims)], axis=0)
        twf = jnp.concatenate([twf_ref[p, s].astype(F32) for s in range(sims)], axis=0)
        deg_p, eps_p = degree[p : p + 1] / modes, eps[p : p + 1] / modes
        sets_a = jnp.concatenate([tbar, deg_p * twf, twf, blank], axis=0)
        sets_b = jnp.concatenate([blank, -(eps_p * twf), blank, blank], axis=0)
        leg = leg_ref[p].astype(F32)
        prev = jnp.concatenate([jnp.zeros_like(leg[:, :1]), leg[:, : rows - 1]], axis=1)
        low, high = lower_f[p : p + 1], upper_f[p : p + 1]
        leg = jnp.concatenate([leg * low, leg * high], axis=0).astype(BF16)
        prev = jnp.concatenate([prev * low, prev * high], axis=0).astype(BF16)
        leg_all[pl.ds(p * span, span), :] = leg
        prev_all[pl.ds(p * span, span), :] = prev
        out_a = dot_t(leg, sets_a.astype(BF16))
        out_b = dot_t(prev, sets_b.astype(BF16))
        for h in range(2):
            small = slots_s[me * pairs + p]
            order = modes - 1 - small if h else small
            norm = jnp.where(order == 0, 1.0, 2.0) * modes ** (-0.5)
            ratio = order.astype(F32) / modes
            rng = slice(h * cycles, (h + 1) * cycles)
            pieces.append((out_a[rng] * (part_a + part_m * ratio) + out_b[rng] * part_b) * norm)
    fourier = jnp.concatenate(pieces, axis=0).astype(BF16)

    base_shape = (block, total)
    row = iota(base_shape, 0)
    base = iota(base_shape, 1) - (mod(row, pairs) * span + div(row, pairs) * cycles)
    place = jnp.concatenate(
        [jnp.where(base == cycle_s[i], 1.0, 0.0) for i in range(cycles)], axis=0
    ).astype(BF16)
    placed = dot(place, fourier).astype(BF16)
    send_f[:, :, : 4 * comps] = placed.reshape(n, block, 4 * comps)

    def exchange(send, recv, s_sem, r_sem):
        copies = []
        for off in range(1, n):
            to = lax.rem(me + off, n)
            copy = pltpu.make_async_remote_copy(
                src_ref=send.at[to], dst_ref=recv.at[me], send_sem=s_sem.at[off],
                recv_sem=r_sem.at[off], device_id={"ma": to},
                device_id_type=pl.DeviceIdType.MESH,
            )
            copy.start()
            copies.append(copy)
        recv[me] = send[me]
        return copies

    pl.semaphore_wait(barrier, n - 1)
    copies = exchange(send_f, recv_f, fs_sem, fr_sem)

    spread_shape = (slots_v.shape[1], n * block)
    col = iota(spread_shape, 1)
    spread = one_hot(
        iota(spread_shape, 0) == div(col, block) * pairs + mod(col, pairs)
    )
    slots = jnp.broadcast_to(slots_v[...], (8, slots_v.shape[1]))
    high_part = div(slots, 256).astype(F32)
    low_part = mod(slots, 256).astype(F32)
    picked = 256.0 * dot(high_part.astype(BF16), spread) + dot(low_part.astype(BF16), spread)
    flip = mod(iota(picked.shape, 1), block) >= pairs
    picked = jnp.where(flip, modes - 1.0 - picked, picked)[0:1]
    select = one_hot(iota((modes, n * block), 0).astype(F32) == picked)

    hs = pixels // LANES * sims
    for load in loads[3:]:
        load.wait()
    moved = dot(table_v[...], select)
    fine_cos, fine_sin = moved[:LANES], moved[LANES : 2 * LANES]
    at = 2 * LANES
    cos_t = moved[at : at + hs] + moved[at + hs : at + 2 * hs]
    sin_t = moved[at + 2 * hs : at + 3 * hs] + moved[at + 3 * hs : at + 4 * hs]
    cos_h, sin_h = cos_t.T, sin_t.T
    synth = jnp.concatenate([fine_cos, fine_sin], axis=1).astype(BF16)
    anal = jnp.concatenate([fine_cos.T, fine_sin.T], axis=0).astype(BF16)

    exp_shape = (4 * comps, 6 * hs)
    ecol = iota(exp_shape, 1)
    which = div(ecol, hs)
    comp_q, comp_c = div(which, 2), mod(which, 2)
    source_c = jnp.where(comp_q == 2, 1 - comp_c, comp_c)
    hit = iota(exp_shape, 0) == comp_q * comps + 2 * mod(ecol, sims) + source_c
    sign = jnp.where(jnp.logical_and(comp_q == 2, comp_c == 0), -1.0, 1.0)
    expand = jnp.where(hit, sign, 0.0).astype(BF16)

    sel_shape = (4 * hs, 4 * comps)
    srow, scol = iota(sel_shape, 0), iota(sel_shape, 1)
    row_q, row_c = div(srow, 2 * hs), mod(div(srow, hs), 2)
    out_g, out_c = div(scol, comps), mod(scol, 2)
    want_q = jnp.where(jnp.logical_or(out_g == 1, out_g == 2), 1, 0)
    swap = out_g >= 2
    want_c = jnp.where(swap, 1 - out_c, out_c)
    same_s = mod(srow, sims) == div(mod(scol, comps), 2)
    negative = jnp.logical_or(
        jnp.logical_and(out_g == 2, out_c == 1), jnp.logical_and(out_g == 3, out_c == 0)
    )
    hit = jnp.logical_and(jnp.logical_and(row_q == want_q, row_c == want_c), same_s)
    gather = jnp.where(hit, jnp.where(negative, -1.0, 1.0), 0.0).astype(BF16)

    mask_t = mask_ref[...].astype(F32).T.astype(BF16)
    m_shape = (pixels // LANES, hs)
    mask = dot(mask_t, one_hot(iota(m_shape, 0) == div(iota(m_shape, 1), sims)))

    lane_shape = (8, total)
    cyc = mod(iota(lane_shape, 1), cycles)
    theta_l = jnp.zeros(lane_shape, F32)
    weight_l = jnp.zeros(lane_shape, F32)
    for r in range(cycles):
        theta_l = jnp.where(cyc == r, colat_s[r], theta_l)
        weight_l = jnp.where(cyc == r, weight_s[r], weight_l)
    with_sin = (weight_l / jnp.sin(theta_l))[0:1]
    with_cos = (weight_l * jnp.cos(theta_l) / jnp.sin(theta_l))[0:1]

    for copy in copies:
        copy.wait_recv()
    got = recv_f[...].reshape(n * block, LANES)[:, : 4 * comps]
    spread_f = dot(got, expand)
    real, imag = [], []
    for q in range(3):
        re = spread_f[:, 2 * q * hs : (2 * q + 1) * hs]
        im = spread_f[:, (2 * q + 1) * hs : (2 * q + 2) * hs]
        real.append((re * cos_h - im * sin_h).astype(BF16))
        imag.append((re * sin_h + im * cos_h).astype(BF16))
    turned = jnp.concatenate(
        [jnp.concatenate(real, axis=1), jnp.concatenate(imag, axis=1)], axis=0
    )
    maps = dot(synth, turned)
    lead = mask * maps[:, :hs]
    products = jnp.concatenate(
        [lead * maps[:, hs : 2 * hs], lead * maps[:, 2 * hs :]], axis=1
    ).astype(BF16)
    half = dot(anal, products)
    parts = []
    count = n * block
    for q in range(2):
        c_part = half[:count, q * hs : (q + 1) * hs]
        s_part = half[count:, q * hs : (q + 1) * hs]
        parts.append((cos_h * c_part + sin_h * s_part).astype(BF16))
        parts.append((cos_h * s_part - sin_h * c_part).astype(BF16))
    spectra = dot(jnp.concatenate(parts, axis=1), gather) * pixels ** (-0.5)
    send_p[:, :, : 4 * comps] = spectra.astype(BF16).reshape(n, block, 4 * comps)
    back = exchange(send_p, recv_p, ps_sem, pr_sem)
    scale = (modes / cycles) ** 0.5 / jnp.sqrt(jnp.maximum(degree * (degree + 1.0), 1.0))
    f_level, f_eps, f_order = degree * scale, eps * scale, orders * scale
    for copy in back:
        copy.wait_recv()

    came = recv_p[...].reshape(n * block, LANES)[:, : 4 * comps].astype(F32).T.astype(BF16)
    by_pair = dot(came, place)
    first = jnp.concatenate([by_pair[: 2 * comps] * with_cos, by_pair[2 * comps :] * with_sin], 0)
    second = by_pair[: 2 * comps] * with_sin
    owner = div(iota((1, total), 1), span)
    keep = [jnp.where(owner == p, 1.0, 0.0) for p in range(pairs)]
    first = jnp.concatenate([(first * keep[p]).astype(BF16) for p in range(pairs)], axis=0)
    second = jnp.concatenate([(second * keep[p]).astype(BF16) for p in range(pairs)], axis=0)
    here = dot(first, leg_all[...])
    before = dot(second, prev_all[...])
    for p in range(pairs):
        a, b = 4 * comps * p, 2 * comps * p
        lev, ep, az = f_level[p : p + 1], f_eps[p : p + 1], f_order[p : p + 1]
        grad = (
            lev * here[a : a + comps] - ep * before[b : b + comps]
            + az * here[a + 2 * comps : a + 3 * comps]
        )
        curl = (
            lev * here[a + comps : a + 2 * comps] - ep * before[b + comps : b + 2 * comps]
            + az * here[a + 3 * comps : a + 4 * comps]
        )
        for s in range(sims):
            grad_ref[p, s] = grad[2 * s : 2 * s + 2]
            curl_ref[p, s] = curl[2 * s : 2 * s + 2]
    for copy in copies + back:
        copy.wait_send()


def fused(tbar_alm, twf_alm, legendre, m_slots, cycle_order, colatitude, cycle_weight, pixel_mask, n):
    pairs, sims, _, rows = tbar_alm.shape
    modes = rows - 1
    cycles = legendre.shape[2]
    pixels = pixel_mask.shape[1]
    total = pairs * 2 * cycles
    by_cycle = jnp.transpose(legendre, (0, 2, 1))
    table = jnp.asarray(split_tables(modes, pixels, sims))
    vmem, smem = pl.BlockSpec(memory_space=pltpu.VMEM), pl.BlockSpec(memory_space=pltpu.SMEM)
    out = pltpu.VMEM(tbar_alm.shape, F32)
    return pl.pallas_call(
        functools.partial(fused_kernel, n, modes, rows, cycles, pixels, sims),
        out_shape=(out, out),
        in_specs=[smem] * 4 + [vmem] + [pl.BlockSpec(memory_space=pl.ANY)] * 5,
        out_specs=(vmem, vmem),
        scratch_shapes=[
            pltpu.VMEM(tbar_alm.shape, BF16),
            pltpu.VMEM(twf_alm.shape, BF16),
            pltpu.VMEM(by_cycle.shape, BF16),
            pltpu.VMEM((pixels // LANES, LANES), jnp.int32),
            pltpu.VMEM(table.shape, BF16),
            pltpu.VMEM((total, rows), BF16),
            pltpu.VMEM((total, rows), BF16),
        ]
        + [pltpu.VMEM((n, 2 * pairs, LANES), BF16)] * 4
        + [pltpu.SemaphoreType.DMA((5,))]
        + [pltpu.SemaphoreType.DMA((n,))] * 4,
        compiler_params=pltpu.CompilerParams(collective_id=0, has_side_effects=True),
        name="estimator",
    )(
        m_slots, cycle_order, colatitude, cycle_weight, m_slots.reshape(1, -1), tbar_alm,
        twf_alm, by_cycle, pixel_mask.reshape(pixels // LANES, LANES), table,
    )


def body(n, *args):
    tbar_alm, legendre, pixel_mask = args[0], args[2], args[7]
    pairs, sims, _, rows = tbar_alm.shape
    cycles = legendre.shape[2]
    fits = (
        pairs == 8
        and cycles % 16 == 0
        and pixel_mask.shape[0] == 1
        and pairs * 2 * cycles <= 512
        and rows <= 1025
        and (pixel_mask.shape[1] // LANES * sims) % LANES == 0
        and sims % 4 == 0
        and all(v & (v - 1) == 0 for v in (sims, cycles, pixel_mask.shape[1]))
    )
    return fused(*args, n) if fits else shards(*args)


def solution(mesh):
    return jax.shard_map(
        functools.partial(body, mesh.shape["ma"]),
        mesh=mesh,
        in_specs=(
            P("ma", "grp", None, None),
            P("ma", "grp", None, None),
            P("ma", None, None),
            P(),
            P(),
            P(),
            P(),
            P("ma", None),
        ),
        out_specs=(P("ma", "grp", None, None), P("ma", "grp", None, None)),
        check_vma=False,
    )
```

profile of v0, /device:TPU:0, one launch (start us, length us, event | category | flops | bytes accessed | tf_op | source)
XLA Modules:
  0.0 19.2 jit_solution(15928283632376012097)
XLA Ops:
  0.6 17.2 %estimator.1 = (f32[8,4,2,257]{3,2,1,0:T(2,128)S(1)}, f32[8,4,2,257]{3,2,1,0:T(2,128)S(1)}) custom-call(s32[128]{0:T(128)} %slots_s.1, s32[16]{0:T(128)} %cycle_s.1, f32[16]{0:T(128)} %colat_s.1, f32[16]{0:T(128)} %weight_s.1, s32[1,128]{1,0:T(1,128)} %bitcast.5, bf16[8,4,2,257]{3,2,1,0:T(2,128)(2,1)} %tbar_hbm.1, bf16[8,4,2,257]{3,2,1,0:T(2,128)(2,1)} %twf_hbm.1, ...), custom_call_target="tpu_custom_call" | custom-call | tf_op jit(solution)/shard_map/estimator/pallas_call | solution.py:461
  17.9 0.6 %copy.13 = f32[8,4,2,257]{3,2,1,0:T(2,128)} copy(f32[8,4,2,257]{3,2,1,0:T(2,128)S(1)} %get-tuple-element.2) | data formatting | bytes 131584
  18.5 0.6 %copy.14 = f32[8,4,2,257]{3,2,1,0:T(2,128)} copy(f32[8,4,2,257]{3,2,1,0:T(2,128)S(1)} %get-tuple-element.3) | data formatting | bytes 131584
where the time goes:
time: 19.3 us; the launch traced here: 19.2 us
  Pallas kernels  17.2 us (89%)
  local copies, waits for them, and re-layouts  1.28 us (7%)
  between operations  0.64 us (3%)
    pallas_call x1, Pallas kernels, fused(): pl.pallas_call(functools.partial(fused_kernel, n, modes, rows, cycles, pi...  17.2 us
    unnamed x2, local copies, waits for them, and re-layouts  1.28 us

commit v1 on v0

--- a/solution.py
+++ b/solution.py
@@ -220,9 +220,10 @@
 
 def fused_kernel(
     n, modes, rows, cycles, pixels, sims,
-    slots_s, cycle_s, colat_s, weight_s, slots_v, tbar_hbm, twf_hbm, leg_hbm, mask_hbm,
-    table_hbm, grad_ref, curl_ref, tbar_ref, twf_ref, leg_ref, mask_ref, table_v, leg_all, prev_all, send_f, recv_f, send_p, recv_p,
-    load_sem, fs_sem, fr_sem, ps_sem, pr_sem,
+    slots_hbm, cycle_hbm, colat_hbm, weight_hbm, row_hbm, tbar_hbm, twf_hbm, leg_hbm, mask_hbm,
+    table_hbm, grad_ref, curl_ref, slots_s, cycle_s, colat_s, weight_s, slots_v,
+    tbar_ref, twf_ref, leg_ref, mask_ref, table_v, leg_all, prev_all, send_f, recv_f, send_p, recv_p,
+    load_sem, move_sem,
 ):
     me = lax.axis_index("ma")
     pairs, padded = tbar_ref.shape[0], rows
@@ -230,22 +231,26 @@
     comps = 2 * sims
     span = 2 * cycles
     total = pairs * span
+    loads = [
+        pltpu.make_async_copy(source, target, load_sem.at[at])
+        for at, (source, target) in enumerate(
+            [(slots_hbm, slots_s), (colat_hbm, colat_s), (cycle_hbm, cycle_s),
+             (leg_hbm, leg_ref), (tbar_hbm, tbar_ref), (twf_hbm, twf_ref),
+             (table_hbm, table_v), (mask_hbm, mask_ref), (row_hbm, slots_v), (weight_hbm, weight_s)]
+        )
+    ]
+    for load in loads[:6]:
+        load.start()
     barrier = pltpu.get_barrier_semaphore()
     for off in range(1, n):
         pl.semaphore_signal(
             barrier, inc=1, device_id={"ma": lax.rem(me + off, n)},
             device_id_type=pl.DeviceIdType.MESH,
         )
-
-    loads = [
-        pltpu.make_async_copy(source, target, load_sem.at[at])
-        for at, (source, target) in enumerate(
-            [(leg_hbm, leg_ref), (tbar_hbm, tbar_ref), (twf_hbm, twf_ref),
-             (table_hbm, table_v), (mask_hbm, mask_ref)]
-        )
-    ]
-    for load in loads:
+    for load in loads[6:]:
         load.start()
+    for load in loads[:3]:
+        load.wait()
 
     row_shape = (pairs, padded)
     smaller = jnp.zeros(row_shape, jnp.int32)
@@ -272,7 +277,7 @@
 
     blank = jnp.zeros((comps, padded), F32)
     pieces = []
-    for load in loads[:3]:
+    for load in loads[3:6]:
         load.wait()
     for p in range(pairs):
         tbar = jnp.concatenate([tbar_ref[p, s].astype(F32) for s in range(sims)], axis=0)
@@ -307,28 +312,30 @@
     placed = dot(place, fourier).astype(BF16)
     send_f[:, :, : 4 * comps] = placed.reshape(n, block, 4 * comps)
 
-    def exchange(send, recv, s_sem, r_sem):
-        copies = []
+    def exchange(send, recv, sem):
         for off in range(1, n):
             to = lax.rem(me + off, n)
-            copy = pltpu.make_async_remote_copy(
-                src_ref=send.at[to], dst_ref=recv.at[me], send_sem=s_sem.at[off],
-                recv_sem=r_sem.at[off], device_id={"ma": to},
+            pltpu.make_async_remote_copy(
+                src_ref=send.at[to], dst_ref=recv.at[me], send_sem=move_sem.at[2 * sem],
+                recv_sem=move_sem.at[2 * sem + 1], device_id={"ma": to},
                 device_id_type=pl.DeviceIdType.MESH,
-            )
-            copy.start()
-            copies.append(copy)
+            ).start()
         recv[me] = send[me]
-        return copies
+
+    def settle(buffer, at):
+        whole = buffer.at[pl.ds(0, n - 1)]
+        pltpu.make_async_copy(whole, whole, move_sem.at[at]).wait()
 
     pl.semaphore_wait(barrier, n - 1)
-    copies = exchange(send_f, recv_f, fs_sem, fr_sem)
+    exchange(send_f, recv_f, 0)
 
     spread_shape = (slots_v.shape[1], n * block)
     col = iota(spread_shape, 1)
     spread = one_hot(
         iota(spread_shape, 0) == div(col, block) * pairs + mod(col, pairs)
     )
+    for load in loads[8:]:
+        load.wait()
     slots = jnp.broadcast_to(slots_v[...], (8, slots_v.shape[1]))
     high_part = div(slots, 256).astype(F32)
     low_part = mod(slots, 256).astype(F32)
@@ -338,7 +345,7 @@
     select = one_hot(iota((modes, n * block), 0).astype(F32) == picked)
 
     hs = pixels // LANES * sims
-    for load in loads[3:]:
+    for load in loads[6:8]:
         load.wait()
     moved = dot(table_v[...], select)
     fine_cos, fine_sin = moved[:LANES], moved[LANES : 2 * LANES]
@@ -386,8 +393,7 @@
     with_sin = (weight_l / jnp.sin(theta_l))[0:1]
     with_cos = (weight_l * jnp.cos(theta_l) / jnp.sin(theta_l))[0:1]
 
-    for copy in copies:
-        copy.wait_recv()
+    settle(recv_f, 1)
     got = recv_f[...].reshape(n * block, LANES)[:, : 4 * comps]
     spread_f = dot(got, expand)
     real, imag = [], []
@@ -414,11 +420,10 @@
         parts.append((cos_h * s_part - sin_h * c_part).astype(BF16))
     spectra = dot(jnp.concatenate(parts, axis=1), gather) * pixels ** (-0.5)
     send_p[:, :, : 4 * comps] = spectra.astype(BF16).reshape(n, block, 4 * comps)
-    back = exchange(send_p, recv_p, ps_sem, pr_sem)
+    exchange(send_p, recv_p, 1)
     scale = (modes / cycles) ** 0.5 / jnp.sqrt(jnp.maximum(degree * (degree + 1.0), 1.0))
     f_level, f_eps, f_order = degree * scale, eps * scale, orders * scale
-    for copy in back:
-        copy.wait_recv()
+    settle(recv_p, 3)
 
     came = recv_p[...].reshape(n * block, LANES)[:, : 4 * comps].astype(F32).T.astype(BF16)
     by_pair = dot(came, place)
@@ -444,8 +449,8 @@
         for s in range(sims):
             grad_ref[p, s] = grad[2 * s : 2 * s + 2]
             curl_ref[p, s] = curl[2 * s : 2 * s + 2]
-    for copy in copies + back:
-        copy.wait_send()
+    settle(send_f, 0)
+    settle(send_p, 2)
 
 
 def fused(tbar_alm, twf_alm, legendre, m_slots, cycle_order, colatitude, cycle_weight, pixel_mask, n):
@@ -456,14 +461,19 @@
     total = pairs * 2 * cycles
     by_cycle = jnp.transpose(legendre, (0, 2, 1))
     table = jnp.asarray(split_tables(modes, pixels, sims))
-    vmem, smem = pl.BlockSpec(memory_space=pltpu.VMEM), pl.BlockSpec(memory_space=pltpu.SMEM)
+    vmem = pl.BlockSpec(memory_space=pltpu.VMEM)
     out = pltpu.VMEM(tbar_alm.shape, F32)
     return pl.pallas_call(
         functools.partial(fused_kernel, n, modes, rows, cycles, pixels, sims),
         out_shape=(out, out),
-        in_specs=[smem] * 4 + [vmem] + [pl.BlockSpec(memory_space=pl.ANY)] * 5,
+        in_specs=[pl.BlockSpec(memory_space=pl.ANY)] * 10,
         out_specs=(vmem, vmem),
         scratch_shapes=[
+            pltpu.SMEM(m_slots.shape, jnp.int32),
+            pltpu.SMEM(cycle_order.shape, jnp.int32),
+            pltpu.SMEM(colatitude.shape, F32),
+            pltpu.SMEM(cycle_weight.shape, F32),
+            pltpu.VMEM((1, m_slots.shape[0]), jnp.int32),
             pltpu.VMEM(tbar_alm.shape, BF16),
             pltpu.VMEM(twf_alm.shape, BF16),
             pltpu.VMEM(by_cycle.shape, BF16),
@@ -473,8 +483,7 @@
             pltpu.VMEM((total, rows), BF16),
         ]
         + [pltpu.VMEM((n, 2 * pairs, LANES), BF16)] * 4
-        + [pltpu.SemaphoreType.DMA((5,))]
-        + [pltpu.SemaphoreType.DMA((n,))] * 4,
+        + [pltpu.SemaphoreType.DMA((10,)), pltpu.SemaphoreType.DMA((4,))],
         compiler_params=pltpu.CompilerParams(collective_id=0, has_side_effects=True),
         name="estimator",
     )(

time: 19.3 us -> 18.1 us (0.938)
  Pallas kernels: 17.2 us -> 16 us
    pallas_call x1, Pallas kernels: 17.2 us -> 16 us  [fused(): pl.pallas_call(functools.partial(fused_kernel, n, modes, rows, cycles, pi...]
where the time goes in v1:
time: 18.1 us; the launch traced here: 17.9 us
  Pallas kernels  16 us (88%)
  local copies, waits for them, and re-layouts  1.28 us (7%)
  between operations  0.64 us (4%)
    pallas_call x1, Pallas kernels, fused(): pl.pallas_call(functools.partial(fused_kernel, n, modes, rows, cycles, pi...  16 us
    unnamed x2, local copies, waits for them, and re-layouts  1.28 us

profile of v1, /device:TPU:0, one launch (start us, length us, event | category | flops | bytes accessed | tf_op | source)
XLA Modules:
  0.0 17.9 jit_solution(5611303381721415159)
XLA Ops:
  0.6 16.0 %estimator.1 = (f32[8,4,2,257]{3,2,1,0:T(2,128)S(1)}, f32[8,4,2,257]{3,2,1,0:T(2,128)S(1)}) custom-call(s32[128]{0:T(128)} %slots_hbm.1, s32[16]{0:T(128)} %cycle_hbm.1, f32[16]{0:T(128)} %colat_hbm.1, f32[16]{0:T(128)} %weight_hbm.1, s32[1,128]{1,0:T(1,128)} %bitcast.5, bf16[8,4,2,257]{3,2,1,0:T(2,128)(2,1)} %tbar_hbm.1, bf16[8,4,2,257]{3,2,1,0:T(2,128)(2,1)} %twf_hbm.1, ...), custom_call_target="tpu_custom_call" | custom-call | tf_op jit(solution)/shard_map/estimator/pallas_call | solution.py:466
  16.6 0.6 %copy.13 = f32[8,4,2,257]{3,2,1,0:T(2,128)} copy(f32[8,4,2,257]{3,2,1,0:T(2,128)S(1)} %get-tuple-element.2) | data formatting | bytes 131584
  17.3 0.6 %copy.14 = f32[8,4,2,257]{3,2,1,0:T(2,128)} copy(f32[8,4,2,257]{3,2,1,0:T(2,128)S(1)} %get-tuple-element.3) | data formatting | bytes 131584

commit v2 on v1

v2 whole, which is shorter than its diff:
```python
import math

import functools

import jax
import jax.numpy as jnp
import numpy as np
from jax import lax
from jax.experimental import pallas as pl
from jax.experimental.pallas import tpu as pltpu
from jax.sharding import PartitionSpec as P


def pair_layout(small_orders, mode_count):
    row_index = lax.broadcasted_iota(jnp.int32, (small_orders.shape[0], mode_count + 1), 1)
    smaller = small_orders[:, None]
    upper_half = row_index >= mode_count - smaller
    degree = jnp.where(upper_half, row_index - 1, smaller + row_index)
    orders = jnp.where(upper_half, mode_count - 1 - smaller, smaller + 0 * row_index)
    return (upper_half, degree.astype(jnp.float32), orders.astype(jnp.float32))


def raising(degree, orders):
    square = (
        (degree * degree - orders * orders)
        * (2.0 * degree + 1.0)
        / jnp.maximum(2.0 * degree - 1.0, 1.0)
    )
    return jnp.where(degree > orders, jnp.sqrt(jnp.where(degree > orders, square, 0.0)), 0.0)


def synthesis_sets(tbar_alm, twf_alm, degree, raising_factor, mode_count):
    wiener = twf_alm.astype(jnp.float32)
    scaled = (raising_factor / mode_count)[:, None, None, :] * wiener
    raised = jnp.concatenate([scaled[..., 1:], jnp.zeros_like(scaled[..., :1])], axis=-1)
    stacked = jnp.stack(
        [
            tbar_alm.astype(jnp.float32),
            wiener,
            (degree / mode_count)[:, None, None, :] * wiener,
            raised,
        ],
        axis=2,
    )
    return stacked.reshape(stacked.shape[0], stacked.shape[1], 8, stacked.shape[4]).astype(
        jnp.bfloat16
    )


def mode_columns(small_orders, mode_count):
    return jnp.stack([small_orders, mode_count - 1 - small_orders], axis=1).reshape(-1)


def fourier_table(orders_int, pixel_count):
    pixel_index = lax.broadcasted_iota(jnp.int32, (orders_int.shape[0], pixel_count), 1)
    turns = orders_int[:, None] * pixel_index % pixel_count
    radians = turns.astype(jnp.float32) * (2.0 * math.pi / pixel_count)
    return jnp.stack([jnp.cos(radians), -jnp.sin(radians)], axis=0).astype(jnp.bfloat16)


def combine_modes(legendre_sums, orders_int, cos_cycle, sin_cycle, mode_count):
    orders_real = orders_int.astype(jnp.float32)
    inv_sin = 1.0 / sin_cycle
    ratio = (orders_real / mode_count)[:, None]
    theta_real = (cos_cycle * legendre_sums[:, 4] - legendre_sums[:, 6]) * inv_sin
    theta_imag = (cos_cycle * legendre_sums[:, 5] - legendre_sums[:, 7]) * inv_sin
    phi_real = -ratio * legendre_sums[:, 3] * inv_sin
    phi_imag = ratio * legendre_sums[:, 2] * inv_sin
    weight = (jnp.where(orders_int == 0, 1.0, 2.0) * mode_count ** (-0.5))[:, None]
    stacked = jnp.stack(
        [legendre_sums[:, 0], legendre_sums[:, 1], theta_real, theta_imag, phi_real, phi_imag],
        axis=1,
    )
    return (stacked * weight).astype(jnp.bfloat16)


def analysis_sets(spectra, colatitude, cycle_weight):
    with_cos = cycle_weight * jnp.cos(colatitude) / jnp.sin(colatitude)
    with_sin = cycle_weight / jnp.sin(colatitude)
    stacked = jnp.stack(
        [
            spectra[:, 0] * with_cos,
            spectra[:, 0] * with_sin,
            spectra[:, 1] * with_cos,
            spectra[:, 1] * with_sin,
        ],
        axis=1,
    )
    return stacked.reshape(spectra.shape[0], 8, spectra.shape[3], spectra.shape[4]).astype(
        jnp.bfloat16
    )


def estimate(merged, degree, orders, raising_factor, mode_count, cycle_count):
    level = degree[:, None, :]
    azimuth = orders[:, None, :]
    factor = raising_factor[:, None, :]

    def previous(values):
        return jnp.concatenate([jnp.zeros_like(values[..., :1]), values[..., :-1]], axis=-1)

    grad_real = (
        level * merged[:, :, 0] - factor * previous(merged[:, :, 2]) + azimuth * merged[:, :, 7]
    )
    grad_imag = (
        level * merged[:, :, 1] - factor * previous(merged[:, :, 3]) - azimuth * merged[:, :, 6]
    )
    curl_real = (
        level * merged[:, :, 4] - factor * previous(merged[:, :, 6]) - azimuth * merged[:, :, 3]
    )
    curl_imag = (
        level * merged[:, :, 5] - factor * previous(merged[:, :, 7]) + azimuth * merged[:, :, 2]
    )
    scale = (mode_count / cycle_count) ** 0.5 / jnp.sqrt(jnp.maximum(level * (level + 1.0), 1.0))
    scale = scale[:, :, None, :]
    return (
        jnp.stack([grad_real, grad_imag], axis=2) * scale,
        jnp.stack([curl_real, curl_imag], axis=2) * scale,
    )


def shards(tbar_alm, twf_alm, legendre, m_slots, cycle_order, colatitude, cycle_weight, pixel_mask):
    pairs_dev = tbar_alm.shape[0]
    row_count = tbar_alm.shape[3]
    mode_count = row_count - 1
    cycle_count = legendre.shape[2]
    cycle_dev = pixel_mask.shape[0]
    pixel_count = pixel_mask.shape[1]
    device_slot = lax.axis_index("ma")
    local_small = lax.dynamic_slice_in_dim(m_slots, device_slot * pairs_dev, pairs_dev)
    upper_half, degree, orders = pair_layout(local_small, mode_count)
    raising_factor = raising(degree, orders)
    coeff_sets = synthesis_sets(tbar_alm, twf_alm, degree, raising_factor, mode_count)
    halves = jnp.stack([jnp.logical_not(upper_half), upper_half], axis=1)
    masked = coeff_sets[:, None] * halves.astype(jnp.bfloat16)[:, :, None, None, :]
    legendre_sums = jnp.einsum(
        "phsck,pkr->scphr", masked, legendre, preferred_element_type=jnp.float32
    )
    legendre_sums = jnp.take(legendre_sums, cycle_order, axis=4)
    legendre_sums = legendre_sums.reshape(legendre_sums.shape[0], 8, 2 * pairs_dev, cycle_count)
    all_orders = mode_columns(m_slots, mode_count)
    dft_table = fourier_table(all_orders, pixel_count)
    pixel_weights = pixel_mask.astype(jnp.float32)
    slot_theta = jnp.take(colatitude, cycle_order)
    local_orders = mode_columns(local_small, mode_count)
    outgoing = combine_modes(
        legendre_sums, local_orders, jnp.cos(slot_theta), jnp.sin(slot_theta), mode_count
    )
    fourier = lax.all_to_all(outgoing, "ma", split_axis=3, concat_axis=2, tiled=True)
    fourier = fourier.reshape(fourier.shape[0], 3, 2, mode_count, cycle_dev)
    cycle_maps = jnp.einsum(
        "sqemr,emj->sqrj", fourier, dft_table, preferred_element_type=jnp.float32
    )
    products = (pixel_weights * cycle_maps[:, 0:1] * cycle_maps[:, 1:3]).astype(jnp.bfloat16)
    spectra = jnp.einsum("sqrj,emj->sqemr", products, dft_table, preferred_element_type=jnp.float32)
    received = (spectra * pixel_count ** (-0.5)).astype(jnp.bfloat16)
    returned = lax.all_to_all(received, "ma", split_axis=3, concat_axis=4, tiled=True)
    inverse = (
        jnp.zeros((cycle_count,), jnp.int32).at[cycle_order].set(lax.iota(jnp.int32, cycle_count))
    )
    spectra = jnp.take(returned, inverse, axis=4).astype(jnp.float32)
    weighted = analysis_sets(spectra, colatitude, cycle_weight)
    weighted = weighted.reshape(weighted.shape[0], 8, pairs_dev, 2, cycle_count)
    projected = jnp.einsum(
        "scphr,pkr->phsck", weighted, legendre, preferred_element_type=jnp.float32
    )
    merged = jnp.sum(projected * halves.astype(jnp.float32)[:, :, None, None, :], axis=1)
    return estimate(merged, degree, orders, raising_factor, mode_count, cycle_count)


LANES = 128
TURNS = 2
F32 = jnp.float32
BF16 = jnp.bfloat16


def split_tables(mode_count, pixel_count, sims):
    high_count = LANES // (TURNS * sims)
    low_count = pixel_count // high_count
    m = np.arange(mode_count)[:, None]
    low = np.arange(low_count)[None, :]
    high = (np.arange(LANES) // sims % high_count)[None, :] * low_count
    fine = (m * low % pixel_count) * (2.0 * math.pi / pixel_count)
    coarse = (m * high % pixel_count) * (2.0 * math.pi / pixel_count)

    def halves(values):
        upper = values.astype(np.float32).astype(BF16)
        return [upper, (values.astype(np.float32) - upper.astype(np.float32)).astype(BF16)]

    waves = [np.cos(fine).astype(BF16), (-np.sin(fine)).astype(BF16)]
    by_pixel = np.concatenate([wave.T for wave in waves], axis=0)
    by_mode = np.concatenate(waves + halves(np.cos(coarse)) + halves(np.sin(coarse)), axis=1)
    return by_pixel, by_mode


def spread_table(sims):
    comps = 2 * sims
    quad = LANES // (4 * comps)
    row = np.arange(TURNS * LANES)[:, None]
    col = np.arange(6 * LANES)[None, :]
    high_count = LANES // (TURNS * sims)
    row_t, row_g, row_s, row_c = row // LANES, row // comps % 4, row // 2 % sims, row % 2
    col_q, col_c = col // (2 * LANES), col // LANES % 2
    col_t, col_s = col % LANES // (high_count * sims), col % sims
    group_q = np.array([0, 1, 2, 1])[row_g]
    source_c = np.where(col_q == 2, 1 - col_c, col_c)
    sign = np.where((col_q == 2) & (col_c == 0), -1.0, 1.0)
    hit = (row_t == col_t) & (row_s == col_s) & (group_q == col_q) & (row_c == source_c)
    return np.where(hit, sign, 0.0).astype(BF16)


def gather_table(sims):
    comps = 2 * sims
    quad = LANES // (4 * comps)
    high_count = LANES // (TURNS * sims)
    row = np.arange(quad * 4 * LANES)[:, None]
    col = np.arange(LANES)[None, :]
    hit = row // (4 * LANES) == col // (2 * comps) % quad
    hit &= row // (2 * LANES) % 2 == col // comps % 2
    hit &= row // LANES % 2 == col % 2
    hit &= row % LANES // (high_count * sims) == col // (2 * comps * quad)
    hit &= row % sims == col // 2 % sims
    return np.where(hit, 1.0, 0.0).astype(BF16)


def iota(shape, axis):
    return lax.broadcasted_iota(jnp.int32, shape, axis)


def div(values, size):
    return values >> (size.bit_length() - 1)


def mod(values, size):
    return values & (size - 1)


def one_hot(condition):
    return jnp.where(condition, 1.0, 0.0).astype(BF16)


def dot(left, right):
    return jnp.dot(left, right, preferred_element_type=F32)


def dot_t(left, right):
    return lax.dot_general(left, right, (((1,), (1,)), ((), ())), preferred_element_type=F32)


def fused_kernel(
    n, modes, rows, cycles, pixels, sims,
    slots_hbm, cycle_hbm, colat_hbm, weight_hbm, row_hbm, tbar_hbm, twf_hbm, leg_hbm, mask_hbm,
    pixel_hbm, mode_hbm, spread_hbm, gather_hbm,
    grad_ref, curl_ref,
    slots_s, cycle_s, colat_s, weight_s, slots_v, tbar_ref, twf_ref, leg_ref, mask_ref,
    pixel_v, mode_v, spread_v, gather_v,
    leg_all, prev_all, fs_ref, place_ref, keep_ref, synth_ref, anal_ref, high_ref, pixmask_ref,
    send_m, recv_m, send_f, recv_f, send_p, recv_p, load_sem, move_sem,
):
    me = lax.axis_index("ma")
    work = n // TURNS
    pairs = tbar_ref.shape[0]
    comps = 2 * sims
    quad = LANES // (4 * comps)
    groups = pairs // quad
    span = 2 * cycles
    total = pairs * span
    count = n * 2 * pairs
    gh = 2 * groups
    high_count = LANES // (TURNS * sims)
    fine = pixels // high_count
    is_worker = me < work

    names = [
        (slots_hbm, slots_s), (colat_hbm, colat_s), (cycle_hbm, cycle_s),
        (leg_hbm, leg_ref), (tbar_hbm, tbar_ref), (twf_hbm, twf_ref),
        (mask_hbm, mask_ref), (weight_hbm, weight_s), (row_hbm, slots_v),
        (mode_hbm, mode_v), (pixel_hbm, pixel_v), (spread_hbm, spread_v), (gather_hbm, gather_v),
    ]
    loads = [
        pltpu.make_async_copy(source, target, load_sem.at[at])
        for at, (source, target) in enumerate(names)
    ]
    for load in loads[:6]:
        load.start()
    barrier = pltpu.get_barrier_semaphore()

    @pl.when(is_worker)
    def _():
        for off in range(1, n):
            pl.semaphore_signal(
                barrier, inc=1, device_id={"ma": lax.rem(me + off, n)},
                device_id_type=pl.DeviceIdType.MESH,
            )

    for load in loads[6:8]:
        load.start()

    @pl.when(is_worker)
    def _():
        for load in loads[8:]:
            load.start()

    def remote(source, target, at, to):
        return pltpu.make_async_remote_copy(
            src_ref=source, dst_ref=target, send_sem=move_sem.at[2 * at],
            recv_sem=move_sem.at[2 * at + 1], device_id={"ma": to},
            device_id_type=pl.DeviceIdType.MESH,
        )

    def settle(buffer, at):
        pltpu.make_async_copy(buffer, buffer, move_sem.at[at]).wait()

    @pl.when(jnp.logical_not(is_worker))
    def _():
        pl.semaphore_wait(barrier, work)
        loads[6].wait()
        send_m[...] = mask_ref[...].astype(F32).astype(BF16)
        remote(send_m, recv_m, 2, me - work).start()

    for load in loads[:3]:
        load.wait()

    row_shape = (pairs, rows)
    smaller = jnp.zeros(row_shape, jnp.int32)
    for p in range(pairs):
        smaller = jnp.where(iota(row_shape, 0) == p, slots_s[me * pairs + p], smaller)
    k = iota(row_shape, 1)
    upper = k >= modes - smaller
    degree = jnp.where(upper, k - 1, smaller + k).astype(F32)
    orders = jnp.where(upper, modes - 1 - smaller, smaller).astype(F32)
    eps = raising(degree, orders)
    upper_f = jnp.where(upper, 1.0, 0.0)
    lower_f = 1.0 - upper_f

    colat = jnp.zeros((cycles, LANES), F32)
    for r in range(cycles):
        colat = jnp.where(iota(colat.shape, 0) == r, colat_s[r], colat)
    csc = 1.0 / jnp.sin(colat)
    cot = jnp.cos(colat) * csc
    lane_group = mod(div(iota(colat.shape, 1), comps), 4)
    base = jnp.where(lane_group == 0, 1.0, jnp.where(lane_group == 1, cot, csc))

    for load in loads[3:6]:
        load.wait()
    lane = iota((8, LANES), 1)
    lane_quad = div(lane, 4 * comps)
    is_phi = mod(div(lane, comps), 4) == 2
    for g in range(groups):
        sets, legs = [], []
        small = jnp.zeros((8, LANES), jnp.int32)
        for q in range(quad):
            p = g * quad + q
            small = jnp.where(lane_quad == q, slots_s[me * pairs + p], small)
            tbar = jnp.concatenate([tbar_ref[p, s].astype(F32) for s in range(sims)], axis=0)
            twf = jnp.concatenate([twf_ref[p, s].astype(F32) for s in range(sims)], axis=0)
            deg_p, eps_p = degree[p : p + 1] / modes, eps[p : p + 1] / modes
            scaled = -(eps_p * twf)
            raised = jnp.concatenate([scaled[:, 1:], jnp.zeros_like(scaled[:, :1])], axis=1)
            sets += [tbar, deg_p * twf, twf, raised]
            leg = leg_ref[p].astype(F32)
            low, high = lower_f[p : p + 1], upper_f[p : p + 1]
            legs += [leg * low, leg * high]
        legs = jnp.concatenate(legs, axis=0).astype(BF16)
        leg_all[pl.ds(g * quad * span, quad * span), :] = legs
        out = dot_t(legs, jnp.concatenate(sets, axis=0).astype(BF16))
        picked = out[:span]
        for q in range(1, quad):
            own = div(iota(picked.shape, 1), 4 * comps) == q
            picked = jnp.where(own, out[q * span : (q + 1) * span], picked)
        for h in range(2):
            order = (modes - 1 - small if h else small)[0:1]
            norm = jnp.where(order == 0, 1.0, 2.0) * modes ** (-0.5)
            norm = jnp.where(is_phi[0:1], norm * (order.astype(F32) / modes), norm)
            fs_ref[:, 2 * g + h, :] = picked[h * cycles : (h + 1) * cycles] * (base * norm)

    for t in range(TURNS):
        for w in range(work):
            send_f[t, w] = fs_ref[cycle_s[w + work * t], :gh, :].astype(BF16)

    @pl.when(is_worker)
    def _():
        pl.semaphore_wait(barrier, work - 1)

    for w in range(work):
        @pl.when(me != w)
        def _():
            remote(send_f.at[:, w], recv_f.at[:, me], 0, w).start()

    own = mod(me, work)
    recv_f[:, me] = send_f[:, own]

    place_shape = (work * gh, total)
    place_row, place_lane = iota(place_shape, 0), iota(place_shape, 1)
    lane_pair, lane_half = div(place_lane, span), mod(div(place_lane, cycles), 2)
    match = mod(place_row, gh) == div(lane_pair, quad) * 2 + lane_half
    slot_row = div(place_row, gh)
    for t in range(TURNS):
        cyc = jnp.zeros(place_shape, jnp.int32)
        for w in range(work):
            cyc = jnp.where(slot_row == w, cycle_s[w + work * t], cyc)
        place_ref[t] = one_hot(jnp.logical_and(match, cyc == mod(place_lane, cycles)))

    loads[7].wait()
    lane_shape = (8, total)
    cyc = mod(iota(lane_shape, 1), cycles)
    theta_l = jnp.zeros(lane_shape, F32)
    weight_l = jnp.zeros(lane_shape, F32)
    for r in range(cycles):
        theta_l = jnp.where(cyc == r, colat_s[r], theta_l)
        weight_l = jnp.where(cyc == r, weight_s[r], weight_l)
    with_sin = weight_l / jnp.sin(theta_l)
    with_cos = weight_l * jnp.cos(theta_l) / jnp.sin(theta_l)
    owner = div(iota(lane_shape, 1), span)
    for p in range(pairs):
        keep_ref[p, 0] = jnp.where(owner == p, with_cos, 0.0)
        keep_ref[p, 1] = jnp.where(owner == p, with_sin, 0.0)
    for p in range(pairs):
        leg = leg_ref[p].astype(F32)
        prev = jnp.concatenate([jnp.zeros_like(leg[:, :1]), leg[:, : rows - 1]], axis=1)
        low, high = lower_f[p : p + 1], upper_f[p : p + 1]
        prev_all[pl.ds(p * span, span), :] = jnp.concatenate(
            [prev * low, prev * high], axis=0
        ).astype(BF16)
    scale = (modes / cycles) ** 0.5 / jnp.sqrt(jnp.maximum(degree * (degree + 1.0), 1.0))
    f_level, f_eps, f_order = degree * scale, eps * scale, orders * scale

    @pl.when(is_worker)
    def _():
        for load in loads[8:]:
            load.wait()
        pair_count = slots_v.shape[1]

        def pair_of(at):
            source, inner = mod(div(at, gh), n), mod(at, gh)
            return source * pairs + div(inner, 2) * quad + div(at, n * gh)

        slots = jnp.broadcast_to(slots_v[...], (pair_count, pair_count)).astype(F32).astype(BF16)
        spread = one_hot(iota((pair_count, count), 0) == pair_of(iota((pair_count, count), 1)))
        spread_t = one_hot(iota((count, pair_count), 1) == pair_of(iota((count, pair_count), 0)))
        by_lane = dot(slots[:16], spread)[0:8]
        by_lane = jnp.where(mod(iota(by_lane.shape, 1), 2) == 1, modes - 1.0 - by_lane, by_lane)
        by_row = dot_t(spread_t, slots)
        by_row = jnp.where(mod(iota(by_row.shape, 0), 2) == 1, modes - 1.0 - by_row, by_row)
        select = one_hot(iota((modes, count), 0).astype(F32) == by_lane[0:1])
        select_t = jnp.concatenate(
            [
                one_hot((iota(by_row.shape, 1) + at).astype(F32) == by_row)
                for at in range(0, modes, pair_count)
            ],
            axis=1,
        )
        moved = dot(pixel_v[...], select).astype(BF16)
        synth_ref[:, :count] = moved[:fine]
        synth_ref[:, count:] = moved[fine:]
        moved = dot(select_t, mode_v[...])
        anal_ref[:count] = moved[:, :fine].astype(BF16)
        anal_ref[count:] = moved[:, fine : 2 * fine].astype(BF16)
        at = 2 * fine
        for part in range(2):
            high_ref[part] = moved[:, at : at + LANES] + moved[:, at + LANES : at + 2 * LANES]
            at += 2 * LANES

        loads[6].wait()
        own_mask = mask_ref[...].astype(F32)
        settle(recv_m, 5)
        both = jnp.concatenate([own_mask, recv_m[...].astype(F32)], axis=0)
        cut = fine // LANES
        wide = (both.shape[0], LANES)
        m_turn = div(iota(wide, 1), high_count * sims)
        m_high = mod(div(iota(wide, 1), sims), high_count)
        first_row = (m_turn * high_count + m_high) * cut
        both_t = both.T.astype(BF16)
        for at in range(cut):
            pixmask_ref[pl.ds(at * LANES, LANES), :] = dot(
                both_t, one_hot(iota(wide, 0) == first_row + at)
            )

        settle(recv_f.at[:, pl.ds(0, n - 1)], 1)
        got = jnp.concatenate(
            [recv_f[t].reshape(n * gh, LANES) for t in range(TURNS)], axis=1
        )
        quarter = mod(div(iota((8, TURNS * LANES), 1), 4 * comps), quad)[0:1]
        got = jnp.concatenate(
            [got * one_hot(quarter == q) for q in range(quad)], axis=0
        )
        spread_f = dot(got, spread_v[...])
        cos_h, sin_h = high_ref[0], high_ref[1]
        real, imag = [], []
        for q in range(3):
            re = spread_f[:, 2 * q * LANES : (2 * q + 1) * LANES]
            im = spread_f[:, (2 * q + 1) * LANES : (2 * q + 2) * LANES]
            real.append((re * cos_h - im * sin_h).astype(BF16))
            imag.append((re * sin_h + im * cos_h).astype(BF16))
        turned = jnp.concatenate(
            [jnp.concatenate(real, axis=1), jnp.concatenate(imag, axis=1)], axis=0
        )
        maps = dot(synth_ref[...], turned)
        lead = pixmask_ref[...] * maps[:, :LANES]
        products = jnp.concatenate(
            [lead * maps[:, LANES : 2 * LANES], lead * maps[:, 2 * LANES :]], axis=1
        ).astype(BF16)
        half = dot(anal_ref[...], products)
        parts = []
        for q in range(2):
            c_part = half[:count, q * LANES : (q + 1) * LANES]
            s_part = half[count:, q * LANES : (q + 1) * LANES]
            parts.append((cos_h * c_part + sin_h * s_part).astype(BF16))
            parts.append((cos_h * s_part - sin_h * c_part).astype(BF16))
        parts = jnp.concatenate(parts, axis=1)
        block = n * gh
        wide = jnp.concatenate(
            [parts[q * block : (q + 1) * block] for q in range(quad)], axis=1
        )
        spectra = dot(wide, gather_v[...]) * pixels ** (-0.5)
        send_p[...] = spectra.astype(BF16).reshape(n, gh, LANES)
        for d in range(work):
            @pl.when(me != d)
            def _():
                remote(send_p.at[d], recv_p.at[me], 1, d).start()
        for d in range(work, n):
            remote(send_p.at[d], recv_p.at[me], 1, d).start()
        recv_p[me] = send_p[me]
        settle(recv_p.at[pl.ds(0, work - 1)], 3)

    @pl.when(jnp.logical_not(is_worker))
    def _():
        settle(recv_p, 3)

    came = recv_p[...].astype(F32).reshape(work * gh, LANES)
    odd = mod(iota(came.shape, 1), 2) == 1
    from_phi = mod(div(iota(came.shape, 1), comps), 2) == 1
    swapped = jnp.where(odd, pltpu.roll(came, 1, 1), pltpu.roll(came, LANES - 1, 1))
    swapped = jnp.where(odd == from_phi, -swapped, swapped)
    turned = [came.T.astype(BF16), swapped.T.astype(BF16)]
    side = LANES // TURNS
    by_pair = sum(
        dot(
            jnp.concatenate([half[t * side : (t + 1) * side] for half in turned], axis=0),
            place_ref[t],
        )
        for t in range(TURNS)
    )
    first, second = [], []
    for p in range(pairs):
        at = p % quad * 2 * comps
        theta, phi = by_pair[at : at + comps], by_pair[at + comps : at + 2 * comps]
        at += side
        theta_i, phi_i = by_pair[at : at + comps], by_pair[at + comps : at + 2 * comps]
        with_cos, with_sin = keep_ref[p, 0], keep_ref[p, 1]
        first += [theta * with_cos, phi * with_cos, phi_i * with_sin, theta_i * with_sin]
        second += [theta * with_sin, phi * with_sin]
    here = dot(jnp.concatenate(first, axis=0).astype(BF16), leg_all[...])
    before = dot(jnp.concatenate(second, axis=0).astype(BF16), prev_all[...])
    for p in range(pairs):
        a, b = 4 * comps * p, 2 * comps * p
        lev, ep, az = f_level[p : p + 1], f_eps[p : p + 1], f_order[p : p + 1]
        grad = (
            lev * here[a : a + comps] - ep * before[b : b + comps]
            + az * here[a + 2 * comps : a + 3 * comps]
        )
        curl = (
            lev * here[a + comps : a + 2 * comps] - ep * before[b + comps : b + 2 * comps]
            + az * here[a + 3 * comps : a + 4 * comps]
        )
        for s in range(sims):
            grad_ref[p, s] = grad[2 * s : 2 * s + 2]
            curl_ref[p, s] = curl[2 * s : 2 * s + 2]

    @pl.when(is_worker)
    def _():
        settle(send_f.at[:, pl.ds(0, work - 1)], 0)
        settle(send_p.at[pl.ds(0, n - 1)], 2)

    @pl.when(jnp.logical_not(is_worker))
    def _():
        loads_left = send_f
        settle(loads_left, 0)
        settle(send_m, 4)


def store_kernel(grad_ref, curl_ref, grad_hbm, curl_hbm, sem):
    copies = [
        pltpu.make_async_copy(grad_ref, grad_hbm, sem.at[0]),
        pltpu.make_async_copy(curl_ref, curl_hbm, sem.at[1]),
    ]
    for copy in copies:
        copy.start()
    for copy in copies:
        copy.wait()


def fused(tbar_alm, twf_alm, legendre, m_slots, cycle_order, colatitude, cycle_weight, pixel_mask, n):
    pairs, sims, _, rows = tbar_alm.shape
    modes = rows - 1
    cycles = legendre.shape[2]
    pixels = pixel_mask.shape[1]
    total = pairs * 2 * cycles
    count = n * 2 * pairs
    work = n // TURNS
    gh = 2 * pairs * 8 * sims // LANES
    fine = pixels * TURNS * sims // LANES
    by_cycle = jnp.transpose(legendre, (0, 2, 1))
    by_pixel, by_mode = split_tables(modes, pixels, sims)
    tables = [jnp.asarray(x) for x in (by_pixel, by_mode, spread_table(sims), gather_table(sims))]
    vmem, anywhere = pl.BlockSpec(memory_space=pltpu.VMEM), pl.BlockSpec(memory_space=pl.ANY)
    out = pltpu.VMEM(tbar_alm.shape, F32)
    mask_shape = (pixels // LANES, LANES)
    made = pl.pallas_call(
        functools.partial(fused_kernel, n, modes, rows, cycles, pixels, sims),
        out_shape=(out, out),
        in_specs=[anywhere] * 13,
        out_specs=(vmem, vmem),
        scratch_shapes=[
            pltpu.SMEM(m_slots.shape, jnp.int32),
            pltpu.SMEM(cycle_order.shape, jnp.int32),
            pltpu.SMEM(colatitude.shape, F32),
            pltpu.SMEM(cycle_weight.shape, F32),
            pltpu.VMEM((1, m_slots.shape[0]), jnp.int32),
            pltpu.VMEM(tbar_alm.shape, BF16),
            pltpu.VMEM(twf_alm.shape, BF16),
            pltpu.VMEM(by_cycle.shape, BF16),
            pltpu.VMEM(mask_shape, jnp.int32),
        ]
        + [pltpu.VMEM(table.shape, BF16) for table in tables]
        + [
            pltpu.VMEM((total, rows), BF16),
            pltpu.VMEM((total, rows), BF16),
            pltpu.VMEM((cycles, 8, LANES), F32),
            pltpu.VMEM((TURNS, work * gh, total), BF16),
            pltpu.VMEM((pairs, 2, 8, total), F32),
            pltpu.VMEM((fine, 2 * count), BF16),
            pltpu.VMEM((2 * count, fine), BF16),
            pltpu.VMEM((2, count, LANES), F32),
            pltpu.VMEM((fine, LANES), F32),
            pltpu.VMEM(mask_shape, BF16),
            pltpu.VMEM(mask_shape, BF16),
            pltpu.VMEM((TURNS, work, gh, LANES), BF16),
            pltpu.VMEM((TURNS, n, gh, LANES), BF16),
            pltpu.VMEM((n, gh, LANES), BF16),
            pltpu.VMEM((work, gh, LANES), BF16),
            pltpu.SemaphoreType.DMA((13,)),
            pltpu.SemaphoreType.DMA((6,)),
        ],
        compiler_params=pltpu.CompilerParams(collective_id=0, has_side_effects=True),
        name="estimator",
    )(
        m_slots, cycle_order, colatitude, cycle_weight, m_slots.reshape(1, -1), tbar_alm,
        twf_alm, by_cycle, pixel_mask.reshape(mask_shape), *tables,
    )
    return pl.pallas_call(
        store_kernel,
        out_shape=(jax.ShapeDtypeStruct(tbar_alm.shape, F32),) * 2,
        in_specs=[vmem] * 2,
        out_specs=[anywhere] * 2,
        scratch_shapes=[pltpu.SemaphoreType.DMA((2,))],
        name="store",
    )(*(pltpu.with_memory_space_constraint(x, pltpu.VMEM) for x in made))


def body(n, *args):
    tbar_alm, legendre, pixel_mask = args[0], args[2], args[7]
    pairs, sims, _, rows = tbar_alm.shape
    cycles = legendre.shape[2]
    pixels = pixel_mask.shape[1]
    fits = (
        pairs == 8
        and cycles == n == 16
        and pixel_mask.shape[0] == 1
        and rows == 257
        and pairs * n == LANES
        and sims == 4
        and pixels == 4096
    )
    return fused(*args, n) if fits else shards(*args)


def solution(mesh):
    return jax.shard_map(
        functools.partial(body, mesh.shape["ma"]),
        mesh=mesh,
        in_specs=(
            P("ma", "grp", None, None),
            P("ma", "grp", None, None),
            P("ma", None, None),
            P(),
            P(),
            P(),
            P(),
            P("ma", None),
        ),
        out_specs=(P("ma", "grp", None, None), P("ma", "grp", None, None)),
        check_vma=False,
    )
```

time: 18.1 us -> 14.8 us (0.82)
  Pallas kernels: 16 us -> 14 us
  local copies, waits for them, and re-layouts: 1.28 us -> 0 us
    pallas_call x1, Pallas kernels: 16 us -> 13.3 us  [fused(): pl.pallas_call(functools.partial(fused_kernel, n, modes, rows, cycles, pi...]
    unnamed x2 -> x0, local copies, waits for them, and re-layouts: 1.28 us -> none
    pallas_call x0 -> x1, Pallas kernels: none -> 0.69 us  [fused(): pl.pallas_call(store_kernel, out_shape=(jax.ShapeDtypeStruct(tbar_alm.sha...]
where the time goes in v2:
time: 14.8 us; the launch traced here: 14.7 us
  Pallas kernels  14 us (95%)
  between operations  0.64 us (4%)
    pallas_call x1, Pallas kernels, fused(): pl.pallas_call(functools.partial(fused_kernel, n, modes, rows, cycles, pi...  13.3 us
    pallas_call x1, Pallas kernels, fused(): pl.pallas_call(store_kernel, out_shape=(jax.ShapeDtypeStruct(tbar_alm.sha...  0.69 us

profile of v2, /device:TPU:0, one launch (start us, length us, event | category | flops | bytes accessed | tf_op | source)
XLA Modules:
  0.0 14.7 jit_solution(13666771488184420231)
XLA Ops:
  0.6 13.3 %estimator.1 = (f32[8,4,2,257]{3,2,1,0:T(2,128)S(1)}, f32[8,4,2,257]{3,2,1,0:T(2,128)S(1)}) custom-call(s32[128]{0:T(128)} %slots_hbm.1, s32[16]{0:T(128)} %cycle_hbm.1, f32[16]{0:T(128)} %colat_hbm.1, f32[16]{0:T(128)} %weight_hbm.1, s32[1,128]{1,0:T(1,128)} %bitcast.5, bf16[8,4,2,257]{3,2,1,0:T(2,128)(2,1)} %tbar_hbm.1, bf16[8,4,2,257]{3,2,1,0:T(2,128)(2,1)} %twf_hbm.1, ...), custom_call_target="tpu_custom_call" | custom-call | tf_op jit(solution)/shard_map/estimator/pallas_call | solution.py:609
  14.0 0.7 %store.1 = (f32[8,4,2,257]{3,2,1,0:T(2,128)}, f32[8,4,2,257]{3,2,1,0:T(2,128)}) custom-call(f32[8,4,2,257]{3,2,1,0:T(2,128)S(1)} %get-tuple-element.4.grad_ref, f32[8,4,2,257]{3,2,1,0:T(2,128)S(1)} %get-tuple-element.5.curl_ref), custom_call_target="tpu_custom_call" | custom-call | tf_op jit(solution)/shard_map/store/pallas_call | solution.py:651

commit v3 on v2

--- a/solution.py
+++ b/solution.py
@@ -169,7 +169,7 @@
 
 
 LANES = 128
-TURNS = 2
+TURNS = 4
 F32 = jnp.float32
 BF16 = jnp.bfloat16
 
@@ -195,11 +195,10 @@
 
 def spread_table(sims):
     comps = 2 * sims
-    quad = LANES // (4 * comps)
-    row = np.arange(TURNS * LANES)[:, None]
+    row = np.arange(LANES)[:, None]
     col = np.arange(6 * LANES)[None, :]
     high_count = LANES // (TURNS * sims)
-    row_t, row_g, row_s, row_c = row // LANES, row // comps % 4, row // 2 % sims, row % 2
+    row_t, row_g, row_s, row_c = row // (4 * comps), row // comps % 4, row // 2 % sims, row % 2
     col_q, col_c = col // (2 * LANES), col // LANES % 2
     col_t, col_s = col % LANES // (high_count * sims), col % sims
     group_q = np.array([0, 1, 2, 1])[row_g]
@@ -211,14 +210,12 @@
 
 def gather_table(sims):
     comps = 2 * sims
-    quad = LANES // (4 * comps)
     high_count = LANES // (TURNS * sims)
-    row = np.arange(quad * 4 * LANES)[:, None]
+    row = np.arange(4 * LANES)[:, None]
     col = np.arange(LANES)[None, :]
-    hit = row // (4 * LANES) == col // (2 * comps) % quad
-    hit &= row // (2 * LANES) % 2 == col // comps % 2
+    hit = row // (2 * LANES) == col // comps % 2
     hit &= row // LANES % 2 == col % 2
-    hit &= row % LANES // (high_count * sims) == col // (2 * comps * quad)
+    hit &= row % LANES // (high_count * sims) == col // (2 * comps) % TURNS
     hit &= row % sims == col // 2 % sims
     return np.where(hit, 1.0, 0.0).astype(BF16)
 
@@ -269,7 +266,12 @@
     gh = 2 * groups
     high_count = LANES // (TURNS * sims)
     fine = pixels // high_count
-    is_worker = me < work
+    wide = quad * TURNS * 2 * comps
+    seat = lax.rem(lax.div(me, 2), work)
+    is_worker = jnp.logical_and(lax.rem(me, 2) == 1, me < 2 * work)
+
+    def slot_of(w, t):
+        return 2 * w + t % 2 + t // 2 * 2 * work
 
     names = [
         (slots_hbm, slots_s), (colat_hbm, colat_s), (cycle_hbm, cycle_s),
@@ -316,7 +318,8 @@
         pl.semaphore_wait(barrier, work)
         loads[6].wait()
         send_m[...] = mask_ref[...].astype(F32).astype(BF16)
-        remote(send_m, recv_m, 2, me - work).start()
+        turn = lax.rem(me, 2) + 2 * lax.div(me, 2 * work)
+        remote(send_m, recv_m.at[turn], 2, 2 * lax.div(lax.rem(me, 2 * work), 2) + 1).start()
 
     for load in loads[:3]:
         load.wait()
@@ -376,19 +379,16 @@
 
     for t in range(TURNS):
         for w in range(work):
-            send_f[t, w] = fs_ref[cycle_s[w + work * t], :gh, :].astype(BF16)
+            send_f[t, w] = fs_ref[cycle_s[slot_of(w, t)], :gh, :].astype(BF16)
 
     @pl.when(is_worker)
     def _():
         pl.semaphore_wait(barrier, work - 1)
 
     for w in range(work):
-        @pl.when(me != w)
+        @pl.when(me != 2 * w + 1)
         def _():
-            remote(send_f.at[:, w], recv_f.at[:, me], 0, w).start()
-
-    own = mod(me, work)
-    recv_f[:, me] = send_f[:, own]
+            remote(send_f.at[:, w], recv_f.at[:, me], 0, 2 * w + 1).start()
 
     place_shape = (work * gh, total)
     place_row, place_lane = iota(place_shape, 0), iota(place_shape, 1)
@@ -398,7 +398,7 @@
     for t in range(TURNS):
         cyc = jnp.zeros(place_shape, jnp.int32)
         for w in range(work):
-            cyc = jnp.where(slot_row == w, cycle_s[w + work * t], cyc)
+            cyc = jnp.where(slot_row == w, cycle_s[slot_of(w, t)], cyc)
         place_ref[t] = one_hot(jnp.logical_and(match, cyc == mod(place_lane, cycles)))
 
     loads[7].wait()
@@ -462,28 +462,34 @@
             at += 2 * LANES
 
         loads[6].wait()
-        own_mask = mask_ref[...].astype(F32)
-        settle(recv_m, 5)
-        both = jnp.concatenate([own_mask, recv_m[...].astype(F32)], axis=0)
+        recv_f[:, me] = send_f[:, seat]
+        recv_m[1] = mask_ref[...].astype(F32).astype(BF16)
+        settle(recv_m.at[pl.ds(0, TURNS - 1)], 5)
+        both = recv_m[...].astype(F32).reshape(TURNS * mask_ref.shape[0], LANES)
         cut = fine // LANES
-        wide = (both.shape[0], LANES)
-        m_turn = div(iota(wide, 1), high_count * sims)
-        m_high = mod(div(iota(wide, 1), sims), high_count)
+        grid = (both.shape[0], LANES)
+        m_turn = div(iota(grid, 1), high_count * sims)
+        m_high = mod(div(iota(grid, 1), sims), high_count)
         first_row = (m_turn * high_count + m_high) * cut
         both_t = both.T.astype(BF16)
         for at in range(cut):
             pixmask_ref[pl.ds(at * LANES, LANES), :] = dot(
-                both_t, one_hot(iota(wide, 0) == first_row + at)
+                both_t, one_hot(iota(grid, 0) == first_row + at)
             )
 
         settle(recv_f.at[:, pl.ds(0, n - 1)], 1)
-        got = jnp.concatenate(
-            [recv_f[t].reshape(n * gh, LANES) for t in range(TURNS)], axis=1
-        )
-        quarter = mod(div(iota((8, TURNS * LANES), 1), 4 * comps), quad)[0:1]
-        got = jnp.concatenate(
-            [got * one_hot(quarter == q) for q in range(quad)], axis=0
-        )
+        turns = [recv_f[t].astype(F32).reshape(n * gh, LANES) for t in range(TURNS)]
+        block_lane = div(iota((n * gh, LANES), 1), 4 * comps)
+        got = []
+        for q in range(quad):
+            row = None
+            for t in range(TURNS):
+                moved_t = turns[t]
+                if t != q:
+                    moved_t = pltpu.roll(moved_t, (t - q) * 4 * comps % LANES, 1)
+                row = moved_t if row is None else jnp.where(block_lane == t, moved_t, row)
+            got.append(row.astype(BF16))
+        got = jnp.concatenate(got, axis=0)
         spread_f = dot(got, spread_v[...])
         cos_h, sin_h = high_ref[0], high_ref[1]
         real, imag = [], []
@@ -507,36 +513,51 @@
             s_part = half[count:, q * LANES : (q + 1) * LANES]
             parts.append((cos_h * c_part + sin_h * s_part).astype(BF16))
             parts.append((cos_h * s_part - sin_h * c_part).astype(BF16))
-        parts = jnp.concatenate(parts, axis=1)
+        spectra = dot(jnp.concatenate(parts, axis=1), gather_v[...]) * pixels ** (-0.5)
         block = n * gh
-        wide = jnp.concatenate(
-            [parts[q * block : (q + 1) * block] for q in range(quad)], axis=1
-        )
-        spectra = dot(wide, gather_v[...]) * pixels ** (-0.5)
-        send_p[...] = spectra.astype(BF16).reshape(n, gh, LANES)
-        for d in range(work):
-            @pl.when(me != d)
-            def _():
-                remote(send_p.at[d], recv_p.at[me], 1, d).start()
-        for d in range(work, n):
-            remote(send_p.at[d], recv_p.at[me], 1, d).start()
-        recv_p[me] = send_p[me]
+        low_half = iota((block, LANES), 1) < LANES // 2
+        packed = [
+            jnp.where(
+                low_half,
+                spectra[2 * v * block : (2 * v + 1) * block],
+                spectra[(2 * v + 1) * block : (2 * v + 2) * block],
+            )
+            for v in range(wide // LANES)
+        ]
+        packed = jnp.concatenate(packed, axis=1).astype(BF16)
+        send_p[...] = packed.reshape(n, gh, wide)
+        for d in range(n):
+            if d % 2 == 0 or d >= 2 * work:
+                remote(send_p.at[d], recv_p.at[seat], 1, d).start()
+            else:
+                @pl.when(me != d)
+                def _():
+                    remote(send_p.at[d], recv_p.at[seat], 1, d).start()
+        recv_p[seat] = send_p[me]
         settle(recv_p.at[pl.ds(0, work - 1)], 3)
 
     @pl.when(jnp.logical_not(is_worker))
     def _():
         settle(recv_p, 3)
 
-    came = recv_p[...].astype(F32).reshape(work * gh, LANES)
+    came = recv_p[...].astype(F32).reshape(work * gh, wide)
     odd = mod(iota(came.shape, 1), 2) == 1
     from_phi = mod(div(iota(came.shape, 1), comps), 2) == 1
-    swapped = jnp.where(odd, pltpu.roll(came, 1, 1), pltpu.roll(came, LANES - 1, 1))
+    swapped = jnp.where(odd, pltpu.roll(came, 1, 1), pltpu.roll(came, wide - 1, 1))
     swapped = jnp.where(odd == from_phi, -swapped, swapped)
     turned = [came.T.astype(BF16), swapped.T.astype(BF16)]
-    side = LANES // TURNS
+    step = 2 * comps
+    side = quad * step
     by_pair = sum(
         dot(
-            jnp.concatenate([half[t * side : (t + 1) * side] for half in turned], axis=0),
+            jnp.concatenate(
+                [
+                    half[(q * TURNS + t) * step : (q * TURNS + t + 1) * step]
+                    for half in turned
+                    for q in range(quad)
+                ],
+                axis=0,
+            ),
             place_ref[t],
         )
         for t in range(TURNS)
@@ -574,8 +595,7 @@
 
     @pl.when(jnp.logical_not(is_worker))
     def _():
-        loads_left = send_f
-        settle(loads_left, 0)
+        settle(send_f, 0)
         settle(send_m, 4)
 
 
@@ -600,6 +620,7 @@
     work = n // TURNS
     gh = 2 * pairs * 8 * sims // LANES
     fine = pixels * TURNS * sims // LANES
+    wide = pairs // (gh // 2) * TURNS * 4 * sims
     by_cycle = jnp.transpose(legendre, (0, 2, 1))
     by_pixel, by_mode = split_tables(modes, pixels, sims)
     tables = [jnp.asarray(x) for x in (by_pixel, by_mode, spread_table(sims), gather_table(sims))]
@@ -634,11 +655,11 @@
             pltpu.VMEM((2, count, LANES), F32),
             pltpu.VMEM((fine, LANES), F32),
             pltpu.VMEM(mask_shape, BF16),
-            pltpu.VMEM(mask_shape, BF16),
+            pltpu.VMEM((TURNS,) + mask_shape, BF16),
             pltpu.VMEM((TURNS, work, gh, LANES), BF16),
             pltpu.VMEM((TURNS, n, gh, LANES), BF16),
-            pltpu.VMEM((n, gh, LANES), BF16),
-            pltpu.VMEM((work, gh, LANES), BF16),
+            pltpu.VMEM((n, gh, wide), BF16),
+            pltpu.VMEM((work, gh, wide), BF16),
             pltpu.SemaphoreType.DMA((13,)),
             pltpu.SemaphoreType.DMA((6,)),
         ],

time: 14.8 us -> 13.9 us (0.939)
  Pallas kernels: 14 us -> 13.1 us
    pallas_call x1, Pallas kernels: 13.3 us -> 12.4 us  [fused(): pl.pallas_call(functools.partial(fused_kernel, n, modes, rows, cycles, pi...]
where the time goes in v3:
time: 13.9 us; the launch traced here: 13.7 us
  Pallas kernels  13.1 us (94%)
  between operations  0.64 us (5%)
    pallas_call x1, Pallas kernels, fused(): pl.pallas_call(functools.partial(fused_kernel, n, modes, rows, cycles, pi...  12.4 us
    pallas_call x1, Pallas kernels, fused(): pl.pallas_call(store_kernel, out_shape=(jax.ShapeDtypeStruct(tbar_alm.sha...  0.69 us

profile of v3, /device:TPU:0, one launch (start us, length us, event | category | flops | bytes accessed | tf_op | source)
XLA Modules:
  0.0 13.7 jit_solution(281581161227102579)
XLA Ops:
  0.6 12.4 %estimator.1 = (f32[8,4,2,257]{3,2,1,0:T(2,128)S(1)}, f32[8,4,2,257]{3,2,1,0:T(2,128)S(1)}) custom-call(s32[128]{0:T(128)} %slots_hbm.1, s32[16]{0:T(128)} %cycle_hbm.1, f32[16]{0:T(128)} %colat_hbm.1, f32[16]{0:T(128)} %weight_hbm.1, s32[1,128]{1,0:T(1,128)} %bitcast.5, bf16[8,4,2,257]{3,2,1,0:T(2,128)(2,1)} %tbar_hbm.1, bf16[8,4,2,257]{3,2,1,0:T(2,128)(2,1)} %twf_hbm.1, ...), custom_call_target="tpu_custom_call" | custom-call | tf_op jit(solution)/shard_map/estimator/pallas_call | solution.py:630
  13.0 0.7 %store.1 = (f32[8,4,2,257]{3,2,1,0:T(2,128)}, f32[8,4,2,257]{3,2,1,0:T(2,128)}) custom-call(f32[8,4,2,257]{3,2,1,0:T(2,128)S(1)} %get-tuple-element.4.grad_ref, f32[8,4,2,257]{3,2,1,0:T(2,128)S(1)} %get-tuple-element.5.curl_ref), custom_call_target="tpu_custom_call" | custom-call | tf_op jit(solution)/shard_map/store/pallas_call | solution.py:672

commit v4 on v3

--- a/solution.py
+++ b/solution.py
@@ -251,7 +251,8 @@
     grad_ref, curl_ref,
     slots_s, cycle_s, colat_s, weight_s, slots_v, tbar_ref, twf_ref, leg_ref, mask_ref,
     pixel_v, mode_v, spread_v, gather_v,
-    leg_all, prev_all, fs_ref, place_ref, keep_ref, synth_ref, anal_ref, high_ref, pixmask_ref,
+    leg_all, prev_all, fs_ref, place_ref, keep_ref, synth_ref, synth_l, anal_ref, anal_c, high_ref,
+    pixmask_ref, maps_ref,
     send_m, recv_m, send_f, recv_f, send_p, recv_p, load_sem, move_sem,
 ):
     me = lax.axis_index("ma")
@@ -268,6 +269,8 @@
     fine = pixels // high_count
     wide = quad * TURNS * 2 * comps
     seat = lax.rem(lax.div(me, 2), work)
+    prompt = n - n // 4
+    first = 2 * gh
     is_worker = jnp.logical_and(lax.rem(me, 2) == 1, me < 2 * work)
 
     def slot_of(w, t):
@@ -303,10 +306,10 @@
         for load in loads[8:]:
             load.start()
 
-    def remote(source, target, at, to):
+    def remote(source, target, at, to, mark=None):
         return pltpu.make_async_remote_copy(
             src_ref=source, dst_ref=target, send_sem=move_sem.at[2 * at],
-            recv_sem=move_sem.at[2 * at + 1], device_id={"ma": to},
+            recv_sem=move_sem.at[2 * at + 1 if mark is None else mark], device_id={"ma": to},
             device_id_type=pl.DeviceIdType.MESH,
         )
 
@@ -385,10 +388,11 @@
     def _():
         pl.semaphore_wait(barrier, work - 1)
 
+    tardy = 1 + 5 * lax.div(me, prompt)
     for w in range(work):
         @pl.when(me != 2 * w + 1)
         def _():
-            remote(send_f.at[:, w], recv_f.at[:, me], 0, 2 * w + 1).start()
+            remote(send_f.at[:, w], recv_f.at[:, me], 0, 2 * w + 1, tardy).start()
 
     place_shape = (work * gh, total)
     place_row, place_lane = iota(place_shape, 0), iota(place_shape, 1)
@@ -431,9 +435,15 @@
             load.wait()
         pair_count = slots_v.shape[1]
 
+        ahead = prompt * gh
+
         def pair_of(at):
-            source, inner = mod(div(at, gh), n), mod(at, gh)
-            return source * pairs + div(inner, 2) * quad + div(at, n * gh)
+            behind = at >= quad * ahead
+            rest = at - quad * ahead
+            early = (at * (65536 // ahead + 1)) >> 16
+            q = jnp.where(behind, div(rest, (n - prompt) * gh), early)
+            inner = jnp.where(behind, ahead + mod(rest, (n - prompt) * gh), at - ahead * early)
+            return div(inner, gh) * pairs + div(mod(inner, gh), 2) * quad + q
 
         slots = jnp.broadcast_to(slots_v[...], (pair_count, pair_count)).astype(F32).astype(BF16)
         spread = one_hot(iota((pair_count, count), 0) == pair_of(iota((pair_count, count), 1)))
@@ -451,11 +461,20 @@
             axis=1,
         )
         moved = dot(pixel_v[...], select).astype(BF16)
-        synth_ref[:, :count] = moved[:fine]
-        synth_ref[:, count:] = moved[fine:]
+        cut_at = quad * ahead
+        synth_ref[...] = jnp.concatenate([moved[:fine, :cut_at], moved[fine:, :cut_at]], axis=1)
+        synth_l[...] = jnp.concatenate([moved[:fine, cut_at:], moved[fine:, cut_at:]], axis=1)
         moved = dot(select_t, mode_v[...])
         anal_ref[:count] = moved[:, :fine].astype(BF16)
         anal_ref[count:] = moved[:, fine : 2 * fine].astype(BF16)
+        anal_c[...] = jnp.concatenate(
+            [
+                moved[q * ahead : q * ahead + first, part * fine : (part + 1) * fine]
+                for part in range(2)
+                for q in range(quad)
+            ],
+            axis=0,
+        ).astype(BF16)
         at = 2 * fine
         for part in range(2):
             high_ref[part] = moved[:, at : at + LANES] + moved[:, at + LANES : at + 2 * LANES]
@@ -477,56 +496,88 @@
                 both_t, one_hot(iota(grid, 0) == first_row + at)
             )
 
-        settle(recv_f.at[:, pl.ds(0, n - 1)], 1)
-        turns = [recv_f[t].astype(F32).reshape(n * gh, LANES) for t in range(TURNS)]
-        block_lane = div(iota((n * gh, LANES), 1), 4 * comps)
-        got = []
-        for q in range(quad):
-            row = None
-            for t in range(TURNS):
-                moved_t = turns[t]
-                if t != q:
-                    moved_t = pltpu.roll(moved_t, (t - q) * 4 * comps % LANES, 1)
-                row = moved_t if row is None else jnp.where(block_lane == t, moved_t, row)
-            got.append(row.astype(BF16))
-        got = jnp.concatenate(got, axis=0)
-        spread_f = dot(got, spread_v[...])
-        cos_h, sin_h = high_ref[0], high_ref[1]
-        real, imag = [], []
-        for q in range(3):
-            re = spread_f[:, 2 * q * LANES : (2 * q + 1) * LANES]
-            im = spread_f[:, (2 * q + 1) * LANES : (2 * q + 2) * LANES]
-            real.append((re * cos_h - im * sin_h).astype(BF16))
-            imag.append((re * sin_h + im * cos_h).astype(BF16))
-        turned = jnp.concatenate(
-            [jnp.concatenate(real, axis=1), jnp.concatenate(imag, axis=1)], axis=0
-        )
-        maps = dot(synth_ref[...], turned)
+        def turn_up(sources, rows_at, size):
+            lanes_of = (size // quad, LANES)
+            turns = [
+                recv_f[t, pl.ds(sources, size // quad // gh)].astype(F32).reshape(lanes_of)
+                for t in range(TURNS)
+            ]
+            block_lane = div(iota(lanes_of, 1), 4 * comps)
+            got = []
+            for q in range(quad):
+                row = None
+                for t in range(TURNS):
+                    moved_t = turns[t]
+                    if t != q:
+                        moved_t = pltpu.roll(moved_t, (t - q) * 4 * comps % LANES, 1)
+                    row = moved_t if row is None else jnp.where(block_lane == t, moved_t, row)
+                got.append(row.astype(BF16))
+            spread_f = dot(jnp.concatenate(got, axis=0), spread_v[...])
+            cos_h, sin_h = high_ref[0, pl.ds(rows_at, size)], high_ref[1, pl.ds(rows_at, size)]
+            real, imag = [], []
+            for q in range(3):
+                re = spread_f[:, 2 * q * LANES : (2 * q + 1) * LANES]
+                im = spread_f[:, (2 * q + 1) * LANES : (2 * q + 2) * LANES]
+                real.append((re * cos_h - im * sin_h).astype(BF16))
+                imag.append((re * sin_h + im * cos_h).astype(BF16))
+            return jnp.concatenate(
+                [jnp.concatenate(real, axis=1), jnp.concatenate(imag, axis=1)], axis=0
+            )
+
+        settle(recv_f.at[:, pl.ds(0, prompt - 1)], 1)
+        maps_ref[...] = dot(synth_ref[...], turn_up(0, 0, cut_at))
+        settle(recv_f.at[:, pl.ds(0, n - prompt)], 6)
+        maps = maps_ref[...] + dot(synth_l[...], turn_up(prompt, cut_at, count - cut_at))
         lead = pixmask_ref[...] * maps[:, :LANES]
         products = jnp.concatenate(
             [lead * maps[:, LANES : 2 * LANES], lead * maps[:, 2 * LANES :]], axis=1
         ).astype(BF16)
-        half = dot(anal_ref[...], products)
-        parts = []
-        for q in range(2):
-            c_part = half[:count, q * LANES : (q + 1) * LANES]
-            s_part = half[count:, q * LANES : (q + 1) * LANES]
-            parts.append((cos_h * c_part + sin_h * s_part).astype(BF16))
-            parts.append((cos_h * s_part - sin_h * c_part).astype(BF16))
-        spectra = dot(jnp.concatenate(parts, axis=1), gather_v[...]) * pixels ** (-0.5)
-        block = n * gh
-        low_half = iota((block, LANES), 1) < LANES // 2
-        packed = [
-            jnp.where(
-                low_half,
-                spectra[2 * v * block : (2 * v + 1) * block],
-                spectra[(2 * v + 1) * block : (2 * v + 2) * block],
+        def bring_down(table, cos_h, sin_h):
+            size = cos_h.shape[0]
+            half = dot(table, products)
+            parts = []
+            for q in range(2):
+                c_part = half[:size, q * LANES : (q + 1) * LANES]
+                s_part = half[size:, q * LANES : (q + 1) * LANES]
+                parts.append((cos_h * c_part + sin_h * s_part).astype(BF16))
+                parts.append((cos_h * s_part - sin_h * c_part).astype(BF16))
+            return dot(jnp.concatenate(parts, axis=1), gather_v[...]) * pixels ** (-0.5)
+
+        def pack(blocks):
+            low_half = iota(blocks[0].shape, 1) < LANES // 2
+            pieces = [
+                jnp.where(low_half, blocks[2 * v], blocks[2 * v + 1])
+                for v in range(wide // LANES)
+            ]
+            whole = jnp.concatenate(pieces, axis=1).astype(BF16)
+            return whole.reshape(whole.shape[0] // gh, gh, wide)
+
+        high_c = [
+            jnp.concatenate([high_ref[part, pl.ds(q * ahead, first)] for q in range(quad)], axis=0)
+            for part in range(2)
+        ]
+        spectra = bring_down(anal_c[...], *high_c)
+        send_p[pl.ds(0, 2)] = pack([spectra[q * first : (q + 1) * first] for q in range(quad)])
+        remote(send_p.at[0], recv_p.at[seat], 1, 0).start()
+
+        @pl.when(me != 1)
+        def _():
+            remote(send_p.at[1], recv_p.at[seat], 1, 1).start()
+
+        spectra = bring_down(anal_ref[...], high_ref[0], high_ref[1])
+        behind = n - prompt
+        blocks = [
+            jnp.concatenate(
+                [
+                    spectra[q * ahead + first : (q + 1) * ahead],
+                    spectra[cut_at + q * behind * gh : cut_at + (q + 1) * behind * gh],
+                ],
+                axis=0,
             )
-            for v in range(wide // LANES)
+            for q in range(quad)
         ]
-        packed = jnp.concatenate(packed, axis=1).astype(BF16)
-        send_p[...] = packed.reshape(n, gh, wide)
-        for d in range(n):
+        send_p[pl.ds(2, n - 2)] = pack(blocks)
+        for d in range(2, n):
             if d % 2 == 0 or d >= 2 * work:
                 remote(send_p.at[d], recv_p.at[seat], 1, d).start()
             else:
@@ -650,10 +701,13 @@
             pltpu.VMEM((cycles, 8, LANES), F32),
             pltpu.VMEM((TURNS, work * gh, total), BF16),
             pltpu.VMEM((pairs, 2, 8, total), F32),
-            pltpu.VMEM((fine, 2 * count), BF16),
+            pltpu.VMEM((fine, 2 * count - count // 2), BF16),
+            pltpu.VMEM((fine, count // 2), BF16),
             pltpu.VMEM((2 * count, fine), BF16),
+            pltpu.VMEM((count // 4, fine), BF16),
             pltpu.VMEM((2, count, LANES), F32),
             pltpu.VMEM((fine, LANES), F32),
+            pltpu.VMEM((fine, 3 * LANES), F32),
             pltpu.VMEM(mask_shape, BF16),
             pltpu.VMEM((TURNS,) + mask_shape, BF16),
             pltpu.VMEM((TURNS, work, gh, LANES), BF16),
@@ -661,7 +715,7 @@
             pltpu.VMEM((n, gh, wide), BF16),
             pltpu.VMEM((work, gh, wide), BF16),
             pltpu.SemaphoreType.DMA((13,)),
-            pltpu.SemaphoreType.DMA((6,)),
+            pltpu.SemaphoreType.DMA((7,)),
         ],
         compiler_params=pltpu.CompilerParams(collective_id=0, has_side_effects=True),
         name="estimator",

time: 13.9 us -> 13.8 us (level)
  no operation moved by 1% of the time
where the time goes in v4:
time: 13.8 us; the launch traced here: 13.6 us
  Pallas kernels  13 us (94%)
  between operations  0.64 us (5%)
    pallas_call x1, Pallas kernels, fused(): pl.pallas_call(functools.partial(fused_kernel, n, modes, rows, cycles, pi...  12.3 us
    pallas_call x1, Pallas kernels, fused(): pl.pallas_call(store_kernel, out_shape=(jax.ShapeDtypeStruct(tbar_alm.sha...  0.69 us

profile of v4, /device:TPU:0, one launch (start us, length us, event | category | flops | bytes accessed | tf_op | source)
XLA Modules:
  0.0 13.6 jit_solution(7852885791227605794)
XLA Ops:
  0.6 12.3 %estimator.1 = (f32[8,4,2,257]{3,2,1,0:T(2,128)S(1)}, f32[8,4,2,257]{3,2,1,0:T(2,128)S(1)}) custom-call(s32[128]{0:T(128)} %slots_hbm.1, s32[16]{0:T(128)} %cycle_hbm.1, f32[16]{0:T(128)} %colat_hbm.1, f32[16]{0:T(128)} %weight_hbm.1, s32[1,128]{1,0:T(1,128)} %bitcast.5, bf16[8,4,2,257]{3,2,1,0:T(2,128)(2,1)} %tbar_hbm.1, bf16[8,4,2,257]{3,2,1,0:T(2,128)(2,1)} %twf_hbm.1, ...), custom_call_target="tpu_custom_call" | custom-call | tf_op jit(solution)/shard_map/estimator/pallas_call | solution.py:681
  12.9 0.7 %store.1 = (f32[8,4,2,257]{3,2,1,0:T(2,128)}, f32[8,4,2,257]{3,2,1,0:T(2,128)}) custom-call(f32[8,4,2,257]{3,2,1,0:T(2,128)S(1)} %get-tuple-element.4.grad_ref, f32[8,4,2,257]{3,2,1,0:T(2,128)S(1)} %get-tuple-element.5.curl_ref), custom_call_target="tpu_custom_call" | custom-call | tf_op jit(solution)/shard_map/store/pallas_call | solution.py:726

commit v5 on v4

--- a/solution.py
+++ b/solution.py
@@ -210,14 +210,15 @@
 
 def gather_table(sims):
     comps = 2 * sims
-    high_count = LANES // (TURNS * sims)
     row = np.arange(4 * LANES)[:, None]
     col = np.arange(LANES)[None, :]
-    hit = row // (2 * LANES) == col // comps % 2
-    hit &= row // LANES % 2 == col % 2
-    hit &= row % LANES // (high_count * sims) == col // (2 * comps) % TURNS
+    group, part = col // comps % 4, col % 2
+    want_q = np.where((group == 1) | (group == 2), 1, 0)
+    want_c = np.where(group >= 2, 1 - part, part)
+    sign = np.where(((group == 2) & (part == 1)) | ((group == 3) & (part == 0)), -1.0, 1.0)
+    hit = (row // (2 * LANES) == want_q) & (row // LANES % 2 == want_c)
     hit &= row % sims == col // 2 % sims
-    return np.where(hit, 1.0, 0.0).astype(BF16)
+    return np.where(hit, sign, 0.0).astype(BF16)
 
 
 def iota(shape, axis):
@@ -251,7 +252,7 @@
     grad_ref, curl_ref,
     slots_s, cycle_s, colat_s, weight_s, slots_v, tbar_ref, twf_ref, leg_ref, mask_ref,
     pixel_v, mode_v, spread_v, gather_v,
-    leg_all, prev_all, fs_ref, place_ref, keep_ref, synth_ref, synth_l, anal_ref, anal_c, high_ref,
+    leg_all, prev_all, leg_p, prev_p, fs_ref, keep_ref, synth_ref, synth_l, anal_ref, anal_c, high_ref,
     pixmask_ref, maps_ref,
     send_m, recv_m, send_f, recv_f, send_p, recv_p, load_sem, move_sem,
 ):
@@ -267,7 +268,6 @@
     gh = 2 * groups
     high_count = LANES // (TURNS * sims)
     fine = pixels // high_count
-    wide = quad * TURNS * 2 * comps
     seat = lax.rem(lax.div(me, 2), work)
     prompt = n - n // 4
     first = 2 * gh
@@ -394,31 +394,30 @@
         def _():
             remote(send_f.at[:, w], recv_f.at[:, me], 0, 2 * w + 1, tardy).start()
 
-    place_shape = (work * gh, total)
-    place_row, place_lane = iota(place_shape, 0), iota(place_shape, 1)
-    lane_pair, lane_half = div(place_lane, span), mod(div(place_lane, cycles), 2)
-    match = mod(place_row, gh) == div(lane_pair, quad) * 2 + lane_half
-    slot_row = div(place_row, gh)
-    for t in range(TURNS):
-        cyc = jnp.zeros(place_shape, jnp.int32)
-        for w in range(work):
-            cyc = jnp.where(slot_row == w, cycle_s[slot_of(w, t)], cyc)
-        place_ref[t] = one_hot(jnp.logical_and(match, cyc == mod(place_lane, cycles)))
-
     loads[7].wait()
-    lane_shape = (8, total)
-    cyc = mod(iota(lane_shape, 1), cycles)
+    lane_shape = (8, LANES)
+    keep_lane = iota(lane_shape, 1)
+    lane_seat = mod(div(keep_lane, gh), TURNS * work)
     theta_l = jnp.zeros(lane_shape, F32)
     weight_l = jnp.zeros(lane_shape, F32)
-    for r in range(cycles):
-        theta_l = jnp.where(cyc == r, colat_s[r], theta_l)
-        weight_l = jnp.where(cyc == r, weight_s[r], weight_l)
+    place_shape = (LANES, total)
+    place_row, place_lane = iota(place_shape, 0), iota(place_shape, 1)
+    row_seat = mod(div(place_row, gh), TURNS * work)
+    row_cycle = jnp.zeros(place_shape, jnp.int32)
+    for t in range(TURNS):
+        for w in range(work):
+            r = cycle_s[slot_of(w, t)]
+            at = t * work + w
+            theta_l = jnp.where(lane_seat == at, colat_s[r], theta_l)
+            weight_l = jnp.where(lane_seat == at, weight_s[r], weight_l)
+            row_cycle = jnp.where(row_seat == at, r, row_cycle)
     with_sin = weight_l / jnp.sin(theta_l)
     with_cos = weight_l * jnp.cos(theta_l) / jnp.sin(theta_l)
-    owner = div(iota(lane_shape, 1), span)
+    lane_g, lane_side = mod(div(keep_lane, 2), groups), div(keep_lane, LANES // 2)
     for p in range(pairs):
-        keep_ref[p, 0] = jnp.where(owner == p, with_cos, 0.0)
-        keep_ref[p, 1] = jnp.where(owner == p, with_sin, 0.0)
+        mine = jnp.logical_and(lane_g == p // quad, lane_side == p % 2)
+        keep_ref[p, 0] = jnp.where(mine, with_cos, 0.0)
+        keep_ref[p, 1] = jnp.where(mine, with_sin, 0.0)
     for p in range(pairs):
         leg = leg_ref[p].astype(F32)
         prev = jnp.concatenate([jnp.zeros_like(leg[:, :1]), leg[:, : rows - 1]], axis=1)
@@ -426,6 +425,14 @@
         prev_all[pl.ds(p * span, span), :] = jnp.concatenate(
             [prev * low, prev * high], axis=0
         ).astype(BF16)
+    row_pair = mod(div(place_row, 2), groups) * quad + div(place_row, LANES // 2)
+    match = jnp.logical_and(
+        row_cycle == mod(place_lane, cycles), mod(place_row, 2) == mod(div(place_lane, cycles), 2)
+    )
+    for k in range(quad // 2):
+        place = one_hot(jnp.logical_and(match, row_pair + 2 * k == div(place_lane, span)))
+        leg_p[k] = dot(place, leg_all[...]).astype(BF16)
+        prev_p[k] = dot(place, prev_all[...]).astype(BF16)
     scale = (modes / cycles) ** 0.5 / jnp.sqrt(jnp.maximum(degree * (degree + 1.0), 1.0))
     f_level, f_eps, f_order = degree * scale, eps * scale, orders * scale
 
@@ -541,99 +548,91 @@
                 s_part = half[size:, q * LANES : (q + 1) * LANES]
                 parts.append((cos_h * c_part + sin_h * s_part).astype(BF16))
                 parts.append((cos_h * s_part - sin_h * c_part).astype(BF16))
-            return dot(jnp.concatenate(parts, axis=1), gather_v[...]) * pixels ** (-0.5)
+            parts = jnp.concatenate(parts, axis=1)
+            turn = mod(div(iota((8, 4 * LANES), 1), LANES // TURNS), TURNS)[0:1]
+            parts = jnp.concatenate([parts * one_hot(turn == t) for t in range(TURNS)], axis=0)
+            return dot(parts, gather_v[...]) * pixels ** (-0.5)
 
         def pack(blocks):
-            low_half = iota(blocks[0].shape, 1) < LANES // 2
-            pieces = [
-                jnp.where(low_half, blocks[2 * v], blocks[2 * v + 1])
-                for v in range(wide // LANES)
-            ]
-            whole = jnp.concatenate(pieces, axis=1).astype(BF16)
-            return whole.reshape(whole.shape[0] // gh, gh, wide)
+            lane_quad = div(iota(blocks[0].shape, 1), 4 * comps)
+            whole = blocks[0]
+            for q in range(1, quad):
+                whole = jnp.where(lane_quad == q, blocks[q], whole)
+            return whole.astype(BF16).reshape(whole.shape[0] // gh, gh, LANES)
 
         high_c = [
             jnp.concatenate([high_ref[part, pl.ds(q * ahead, first)] for q in range(quad)], axis=0)
             for part in range(2)
         ]
         spectra = bring_down(anal_c[...], *high_c)
-        send_p[pl.ds(0, 2)] = pack([spectra[q * first : (q + 1) * first] for q in range(quad)])
-        remote(send_p.at[0], recv_p.at[seat], 1, 0).start()
+        for t in range(TURNS):
+            at = t * quad * first
+            send_p[t, pl.ds(0, 2)] = pack(
+                [spectra[at + q * first : at + (q + 1) * first] for q in range(quad)]
+            )
+        remote(send_p.at[:, 0], recv_p.at[:, seat], 1, 0).start()
 
         @pl.when(me != 1)
         def _():
-            remote(send_p.at[1], recv_p.at[seat], 1, 1).start()
+            remote(send_p.at[:, 1], recv_p.at[:, seat], 1, 1).start()
 
         spectra = bring_down(anal_ref[...], high_ref[0], high_ref[1])
         behind = n - prompt
-        blocks = [
-            jnp.concatenate(
-                [
-                    spectra[q * ahead + first : (q + 1) * ahead],
-                    spectra[cut_at + q * behind * gh : cut_at + (q + 1) * behind * gh],
-                ],
-                axis=0,
-            )
-            for q in range(quad)
-        ]
-        send_p[pl.ds(2, n - 2)] = pack(blocks)
+        for t in range(TURNS):
+            at = t * count
+            late = at + cut_at
+            rest = [
+                jnp.concatenate(
+                    [
+                        spectra[at + q * ahead + first : at + (q + 1) * ahead],
+                        spectra[late + q * behind * gh : late + (q + 1) * behind * gh],
+                    ],
+                    axis=0,
+                )
+                for q in range(quad)
+            ]
+            send_p[t, pl.ds(2, n - 2)] = pack(rest)
         for d in range(2, n):
             if d % 2 == 0 or d >= 2 * work:
-                remote(send_p.at[d], recv_p.at[seat], 1, d).start()
+                remote(send_p.at[:, d], recv_p.at[:, seat], 1, d).start()
             else:
                 @pl.when(me != d)
                 def _():
-                    remote(send_p.at[d], recv_p.at[seat], 1, d).start()
-        recv_p[seat] = send_p[me]
-        settle(recv_p.at[pl.ds(0, work - 1)], 3)
+                    remote(send_p.at[:, d], recv_p.at[:, seat], 1, d).start()
+        recv_p[:, seat] = send_p[:, me]
+        settle(recv_p.at[:, pl.ds(0, work - 1)], 3)
 
     @pl.when(jnp.logical_not(is_worker))
     def _():
         settle(recv_p, 3)
 
-    came = recv_p[...].astype(F32).reshape(work * gh, wide)
-    odd = mod(iota(came.shape, 1), 2) == 1
-    from_phi = mod(div(iota(came.shape, 1), comps), 2) == 1
-    swapped = jnp.where(odd, pltpu.roll(came, 1, 1), pltpu.roll(came, wide - 1, 1))
-    swapped = jnp.where(odd == from_phi, -swapped, swapped)
-    turned = [came.T.astype(BF16), swapped.T.astype(BF16)]
-    step = 2 * comps
-    side = quad * step
-    by_pair = sum(
-        dot(
-            jnp.concatenate(
-                [
-                    half[(q * TURNS + t) * step : (q * TURNS + t + 1) * step]
-                    for half in turned
-                    for q in range(quad)
-                ],
-                axis=0,
-            ),
-            place_ref[t],
-        )
-        for t in range(TURNS)
-    )
-    first, second = [], []
+    came = recv_p[...].astype(F32).reshape(TURNS * work * gh, LANES)
+    came = jnp.concatenate([came, came], axis=0).T
+    here, before = {}, {}
+    for k in range(quad // 2):
+        members = [p for p in range(pairs) if p % quad // 2 == k]
+        first_k, second_k = [], []
+        for p in members:
+            at = p % quad * 4 * comps
+            four = [came[at + g * comps : at + (g + 1) * comps] for g in range(4)]
+            with_cos, with_sin = keep_ref[p, 0], keep_ref[p, 1]
+            first_k += [four[0] * with_cos, four[1] * with_cos]
+            first_k += [four[2] * with_sin, four[3] * with_sin]
+            second_k += [four[0] * with_sin, four[1] * with_sin]
+        out_a = dot(jnp.concatenate(first_k, axis=0).astype(BF16), leg_p[k])
+        out_b = dot(jnp.concatenate(second_k, axis=0).astype(BF16), prev_p[k])
+        for at, p in enumerate(members):
+            here[p] = out_a[at * 4 * comps : (at + 1) * 4 * comps]
+            before[p] = out_b[at * 2 * comps : (at + 1) * 2 * comps]
     for p in range(pairs):
-        at = p % quad * 2 * comps
-        theta, phi = by_pair[at : at + comps], by_pair[at + comps : at + 2 * comps]
-        at += side
-        theta_i, phi_i = by_pair[at : at + comps], by_pair[at + comps : at + 2 * comps]
-        with_cos, with_sin = keep_ref[p, 0], keep_ref[p, 1]
-        first += [theta * with_cos, phi * with_cos, phi_i * with_sin, theta_i * with_sin]
-        second += [theta * with_sin, phi * with_sin]
-    here = dot(jnp.concatenate(first, axis=0).astype(BF16), leg_all[...])
-    before = dot(jnp.concatenate(second, axis=0).astype(BF16), prev_all[...])
-    for p in range(pairs):
-        a, b = 4 * comps * p, 2 * comps * p
         lev, ep, az = f_level[p : p + 1], f_eps[p : p + 1], f_order[p : p + 1]
         grad = (
-            lev * here[a : a + comps] - ep * before[b : b + comps]
-            + az * here[a + 2 * comps : a + 3 * comps]
+            lev * here[p][:comps] - ep * before[p][:comps]
+            + az * here[p][2 * comps : 3 * comps]
         )
         curl = (
-            lev * here[a + comps : a + 2 * comps] - ep * before[b + comps : b + 2 * comps]
-            + az * here[a + 3 * comps : a + 4 * comps]
+            lev * here[p][comps : 2 * comps] - ep * before[p][comps:]
+            + az * here[p][3 * comps :]
         )
         for s in range(sims):
             grad_ref[p, s] = grad[2 * s : 2 * s + 2]
@@ -642,7 +641,7 @@
     @pl.when(is_worker)
     def _():
         settle(send_f.at[:, pl.ds(0, work - 1)], 0)
-        settle(send_p.at[pl.ds(0, n - 1)], 2)
+        settle(send_p.at[:, pl.ds(0, n - 1)], 2)
 
     @pl.when(jnp.logical_not(is_worker))
     def _():
@@ -671,7 +670,6 @@
     work = n // TURNS
     gh = 2 * pairs * 8 * sims // LANES
     fine = pixels * TURNS * sims // LANES
-    wide = pairs // (gh // 2) * TURNS * 4 * sims
     by_cycle = jnp.transpose(legendre, (0, 2, 1))
     by_pixel, by_mode = split_tables(modes, pixels, sims)
     tables = [jnp.asarray(x) for x in (by_pixel, by_mode, spread_table(sims), gather_table(sims))]
@@ -698,9 +696,10 @@
         + [
             pltpu.VMEM((total, rows), BF16),
             pltpu.VMEM((total, rows), BF16),
+            pltpu.VMEM((total // LANES, LANES, rows), BF16),
+            pltpu.VMEM((total // LANES, LANES, rows), BF16),
             pltpu.VMEM((cycles, 8, LANES), F32),
-            pltpu.VMEM((TURNS, work * gh, total), BF16),
-            pltpu.VMEM((pairs, 2, 8, total), F32),
+            pltpu.VMEM((pairs, 2, 8, LANES), F32),
             pltpu.VMEM((fine, 2 * count - count // 2), BF16),
             pltpu.VMEM((fine, count // 2), BF16),
             pltpu.VMEM((2 * count, fine), BF16),
@@ -712,8 +711,8 @@
             pltpu.VMEM((TURNS,) + mask_shape, BF16),
             pltpu.VMEM((TURNS, work, gh, LANES), BF16),
             pltpu.VMEM((TURNS, n, gh, LANES), BF16),
-            pltpu.VMEM((n, gh, wide), BF16),
-            pltpu.VMEM((work, gh, wide), BF16),
+            pltpu.VMEM((TURNS, n, gh, LANES), BF16),
+            pltpu.VMEM((TURNS, work, gh, LANES), BF16),
             pltpu.SemaphoreType.DMA((13,)),
             pltpu.SemaphoreType.DMA((7,)),
         ],

time: 13.8 us -> 13.5 us (0.978)
  Pallas kernels: 13 us -> 12.7 us
    pallas_call x1, Pallas kernels: 12.3 us -> 12 us  [fused(): pl.pallas_call(functools.partial(fused_kernel, n, modes, rows, cycles, pi...]
where the time goes in v5:
time: 13.5 us; the launch traced here: 13.3 us
  Pallas kernels  12.7 us (94%)
  between operations  0.64 us (5%)
    pallas_call x1, Pallas kernels, fused(): pl.pallas_call(functools.partial(fused_kernel, n, modes, rows, cycles, pi...  12 us
    pallas_call x1, Pallas kernels, fused(): pl.pallas_call(store_kernel, out_shape=(jax.ShapeDtypeStruct(tbar_alm.sha...  0.69 us

profile of v5, /device:TPU:0, one launch (start us, length us, event | category | flops | bytes accessed | tf_op | source)
XLA Modules:
  0.0 13.3 jit_solution(8402947941908072033)
XLA Ops:
  0.6 12.0 %estimator.1 = (f32[8,4,2,257]{3,2,1,0:T(2,128)S(1)}, f32[8,4,2,257]{3,2,1,0:T(2,128)S(1)}) custom-call(s32[128]{0:T(128)} %slots_hbm.1, s32[16]{0:T(128)} %cycle_hbm.1, f32[16]{0:T(128)} %colat_hbm.1, f32[16]{0:T(128)} %weight_hbm.1, s32[1,128]{1,0:T(1,128)} %bitcast.5, bf16[8,4,2,257]{3,2,1,0:T(2,128)(2,1)} %tbar_hbm.1, bf16[8,4,2,257]{3,2,1,0:T(2,128)(2,1)} %twf_hbm.1, ...), custom_call_target="tpu_custom_call" | custom-call | tf_op jit(solution)/shard_map/estimator/pallas_call | solution.py:679
  12.6 0.7 %store.1 = (f32[8,4,2,257]{3,2,1,0:T(2,128)}, f32[8,4,2,257]{3,2,1,0:T(2,128)}) custom-call(f32[8,4,2,257]{3,2,1,0:T(2,128)S(1)} %get-tuple-element.4.grad_ref, f32[8,4,2,257]{3,2,1,0:T(2,128)S(1)} %get-tuple-element.5.curl_ref), custom_call_target="tpu_custom_call" | custom-call | tf_op jit(solution)/shard_map/store/pallas_call | solution.py:725

commit v6 on v5

--- a/solution.py
+++ b/solution.py
@@ -490,19 +490,6 @@
         loads[6].wait()
         recv_f[:, me] = send_f[:, seat]
         recv_m[1] = mask_ref[...].astype(F32).astype(BF16)
-        settle(recv_m.at[pl.ds(0, TURNS - 1)], 5)
-        both = recv_m[...].astype(F32).reshape(TURNS * mask_ref.shape[0], LANES)
-        cut = fine // LANES
-        grid = (both.shape[0], LANES)
-        m_turn = div(iota(grid, 1), high_count * sims)
-        m_high = mod(div(iota(grid, 1), sims), high_count)
-        first_row = (m_turn * high_count + m_high) * cut
-        both_t = both.T.astype(BF16)
-        for at in range(cut):
-            pixmask_ref[pl.ds(at * LANES, LANES), :] = dot(
-                both_t, one_hot(iota(grid, 0) == first_row + at)
-            )
-
         def turn_up(sources, rows_at, size):
             lanes_of = (size // quad, LANES)
             turns = [
@@ -533,7 +520,19 @@
 
         settle(recv_f.at[:, pl.ds(0, prompt - 1)], 1)
         maps_ref[...] = dot(synth_ref[...], turn_up(0, 0, cut_at))
+        settle(recv_m.at[pl.ds(0, TURNS - 1)], 5)
         settle(recv_f.at[:, pl.ds(0, n - prompt)], 6)
+        both = recv_m[...].astype(F32).reshape(TURNS * mask_ref.shape[0], LANES)
+        cut = fine // LANES
+        grid = (both.shape[0], LANES)
+        m_turn = div(iota(grid, 1), high_count * sims)
+        m_high = mod(div(iota(grid, 1), sims), high_count)
+        first_row = (m_turn * high_count + m_high) * cut
+        both_t = both.T.astype(BF16)
+        for at in range(cut):
+            pixmask_ref[pl.ds(at * LANES, LANES), :] = dot(
+                both_t, one_hot(iota(grid, 0) == first_row + at)
+            )
         maps = maps_ref[...] + dot(synth_l[...], turn_up(prompt, cut_at, count - cut_at))
         lead = pixmask_ref[...] * maps[:, :LANES]
         products = jnp.concatenate(

time: 13.5 us -> 13.1 us (0.970)
  Pallas kernels: 12.7 us -> 12.3 us
    pallas_call x1, Pallas kernels: 12 us -> 11.7 us  [fused(): pl.pallas_call(functools.partial(fused_kernel, n, modes, rows, cycles, pi...]
where the time goes in v6:
time: 13.1 us; the launch traced here: 13 us
  Pallas kernels  12.3 us (94%)
  between operations  0.64 us (5%)
    pallas_call x1, Pallas kernels, fused(): pl.pallas_call(functools.partial(fused_kernel, n, modes, rows, cycles, pi...  11.7 us
    pallas_call x1, Pallas kernels, fused(): pl.pallas_call(store_kernel, out_shape=(jax.ShapeDtypeStruct(tbar_alm.sha...  0.69 us

profile of v6, /device:TPU:0, one launch (start us, length us, event | category | flops | bytes accessed | tf_op | source)
XLA Modules:
  0.0 13.0 jit_solution(17723509898987340266)
XLA Ops:
  0.6 11.7 %estimator.1 = (f32[8,4,2,257]{3,2,1,0:T(2,128)S(1)}, f32[8,4,2,257]{3,2,1,0:T(2,128)S(1)}) custom-call(s32[128]{0:T(128)} %slots_hbm.1, s32[16]{0:T(128)} %cycle_hbm.1, f32[16]{0:T(128)} %colat_hbm.1, f32[16]{0:T(128)} %weight_hbm.1, s32[1,128]{1,0:T(1,128)} %bitcast.5, bf16[8,4,2,257]{3,2,1,0:T(2,128)(2,1)} %tbar_hbm.1, bf16[8,4,2,257]{3,2,1,0:T(2,128)(2,1)} %twf_hbm.1, ...), custom_call_target="tpu_custom_call" | custom-call | tf_op jit(solution)/shard_map/estimator/pallas_call | solution.py:678
  12.3 0.7 %store.1 = (f32[8,4,2,257]{3,2,1,0:T(2,128)}, f32[8,4,2,257]{3,2,1,0:T(2,128)}) custom-call(f32[8,4,2,257]{3,2,1,0:T(2,128)S(1)} %get-tuple-element.4.grad_ref, f32[8,4,2,257]{3,2,1,0:T(2,128)S(1)} %get-tuple-element.5.curl_ref), custom_call_target="tpu_custom_call" | custom-call | tf_op jit(solution)/shard_map/store/pallas_call | solution.py:724

commit v7 on v6

--- a/solution.py
+++ b/solution.py
@@ -195,12 +195,11 @@
 
 def spread_table(sims):
     comps = 2 * sims
-    row = np.arange(LANES)[:, None]
-    col = np.arange(6 * LANES)[None, :]
-    high_count = LANES // (TURNS * sims)
-    row_t, row_g, row_s, row_c = row // (4 * comps), row // comps % 4, row // 2 % sims, row % 2
-    col_q, col_c = col // (2 * LANES), col // LANES % 2
-    col_t, col_s = col % LANES // (high_count * sims), col % sims
+    row = np.arange(2 * LANES)[:, None]
+    col = np.arange(4 * LANES)[None, :]
+    row_t, row_g, row_s, row_c = row // LANES, row // comps % 4, row // 2 % sims, row % 2
+    col_t, col_s, col_c = col // (LANES // 2) % 2, col % sims, col // LANES % 2
+    col_q = np.where(col < 2 * LANES, 0, 1 + col // (LANES // 4) % 2)
     group_q = np.array([0, 1, 2, 1])[row_g]
     source_c = np.where(col_q == 2, 1 - col_c, col_c)
     sign = np.where((col_q == 2) & (col_c == 0), -1.0, 1.0)
@@ -216,9 +215,11 @@
     want_q = np.where((group == 1) | (group == 2), 1, 0)
     want_c = np.where(group >= 2, 1 - part, part)
     sign = np.where(((group == 2) & (part == 1)) | ((group == 3) & (part == 0)), -1.0, 1.0)
-    hit = (row // (2 * LANES) == want_q) & (row // LANES % 2 == want_c)
+    hit = (row // (LANES // 4) % 2 == want_q) & (row // LANES % 2 == want_c)
     hit &= row % sims == col // 2 % sims
-    return np.where(hit, sign, 0.0).astype(BF16)
+    turn = 2 * (row // (2 * LANES)) + row // (LANES // 2) % 2
+    own = hit & (turn == col // (4 * comps))
+    return np.concatenate([np.where(x, sign, 0.0) for x in (hit, own)], axis=1).astype(BF16)
 
 
 def iota(shape, axis):
@@ -253,7 +254,7 @@
     slots_s, cycle_s, colat_s, weight_s, slots_v, tbar_ref, twf_ref, leg_ref, mask_ref,
     pixel_v, mode_v, spread_v, gather_v,
     leg_all, prev_all, leg_p, prev_p, fs_ref, keep_ref, synth_ref, synth_l, anal_ref, anal_c, high_ref,
-    pixmask_ref, maps_ref,
+    pixmask_ref, maps_ref, pick_ref,
     send_m, recv_m, send_f, recv_f, send_p, recv_p, load_sem, move_sem,
 ):
     me = lax.axis_index("ma")
@@ -347,6 +348,11 @@
     lane_group = mod(div(iota(colat.shape, 1), comps), 4)
     base = jnp.where(lane_group == 0, 1.0, jnp.where(lane_group == 1, cot, csc))
 
+    halves = [
+        [jnp.broadcast_to(part[p : p + 1], (cycles, rows)).astype(BF16) for part in (lower_f, upper_f)]
+        for p in range(pairs)
+    ]
+
     for load in loads[3:6]:
         load.wait()
     lane = iota((8, LANES), 1)
@@ -364,10 +370,8 @@
             scaled = -(eps_p * twf)
             raised = jnp.concatenate([scaled[:, 1:], jnp.zeros_like(scaled[:, :1])], axis=1)
             sets += [tbar, deg_p * twf, twf, raised]
-            leg = leg_ref[p].astype(F32)
-            low, high = lower_f[p : p + 1], upper_f[p : p + 1]
-            legs += [leg * low, leg * high]
-        legs = jnp.concatenate(legs, axis=0).astype(BF16)
+            legs += [leg_ref[p] * part for part in halves[p]]
+        legs = jnp.concatenate(legs, axis=0)
         leg_all[pl.ds(g * quad * span, quad * span), :] = legs
         out = dot_t(legs, jnp.concatenate(sets, axis=0).astype(BF16))
         picked = out[:span]
@@ -378,18 +382,18 @@
             order = (modes - 1 - small if h else small)[0:1]
             norm = jnp.where(order == 0, 1.0, 2.0) * modes ** (-0.5)
             norm = jnp.where(is_phi[0:1], norm * (order.astype(F32) / modes), norm)
-            fs_ref[:, 2 * g + h, :] = picked[h * cycles : (h + 1) * cycles] * (base * norm)
+            fs_ref[pl.ds((2 * g + h) * cycles, cycles), :] = picked[h * cycles : (h + 1) * cycles] * (base * norm)
 
     for t in range(TURNS):
         for w in range(work):
-            send_f[t, w] = fs_ref[cycle_s[slot_of(w, t)], :gh, :].astype(BF16)
+            send_f[t, w] = fs_ref[pl.ds(cycle_s[slot_of(w, t)], gh, stride=cycles), :].astype(BF16)
 
     @pl.when(is_worker)
     def _():
         pl.semaphore_wait(barrier, work - 1)
 
     tardy = 1 + 5 * lax.div(me, prompt)
-    for w in range(work):
+    for w in reversed(range(work)):
         @pl.when(me != 2 * w + 1)
         def _():
             remote(send_f.at[:, w], recv_f.at[:, me], 0, 2 * w + 1, tardy).start()
@@ -489,31 +493,36 @@
 
         loads[6].wait()
         recv_f[:, me] = send_f[:, seat]
+        cut = fine // LANES
+        grid = (TURNS * mask_ref.shape[0], LANES)
+        m_turn = div(iota(grid, 1), LANES // 2)
+        m_high = mod(div(iota(grid, 1), sims), high_count)
+        for j in range(TURNS // 2):
+            first_row = ((m_turn + 2 * j) * high_count + m_high) * cut
+            for at in range(cut):
+                pick_ref[j, at] = one_hot(iota(grid, 0) == first_row + at)
         recv_m[1] = mask_ref[...].astype(F32).astype(BF16)
+        quarter = mod(div(iota((8, 2 * LANES), 1), 4 * comps), quad)[0:1]
+
         def turn_up(sources, rows_at, size):
-            lanes_of = (size // quad, LANES)
             turns = [
-                recv_f[t, pl.ds(sources, size // quad // gh)].astype(F32).reshape(lanes_of)
+                recv_f[t, pl.ds(sources, size // quad // gh)].reshape(size // quad, LANES)
                 for t in range(TURNS)
             ]
-            block_lane = div(iota(lanes_of, 1), 4 * comps)
-            got = []
-            for q in range(quad):
-                row = None
-                for t in range(TURNS):
-                    moved_t = turns[t]
-                    if t != q:
-                        moved_t = pltpu.roll(moved_t, (t - q) * 4 * comps % LANES, 1)
-                    row = moved_t if row is None else jnp.where(block_lane == t, moved_t, row)
-                got.append(row.astype(BF16))
+            pairs_of = [
+                jnp.concatenate(turns[2 * j : 2 * j + 2], axis=1) for j in range(TURNS // 2)
+            ]
+            got = [pair * one_hot(quarter == q) for pair in pairs_of for q in range(quad)]
             spread_f = dot(jnp.concatenate(got, axis=0), spread_v[...])
             cos_h, sin_h = high_ref[0, pl.ds(rows_at, size)], high_ref[1, pl.ds(rows_at, size)]
             real, imag = [], []
-            for q in range(3):
-                re = spread_f[:, 2 * q * LANES : (2 * q + 1) * LANES]
-                im = spread_f[:, (2 * q + 1) * LANES : (2 * q + 2) * LANES]
-                real.append((re * cos_h - im * sin_h).astype(BF16))
-                imag.append((re * sin_h + im * cos_h).astype(BF16))
+            for j in range(TURNS // 2):
+                for kind in range(2):
+                    at = 2 * kind * LANES
+                    re = spread_f[j * size : (j + 1) * size, at : at + LANES]
+                    im = spread_f[j * size : (j + 1) * size, at + LANES : at + 2 * LANES]
+                    real.append((re * cos_h - im * sin_h).astype(BF16))
+                    imag.append((re * sin_h + im * cos_h).astype(BF16))
             return jnp.concatenate(
                 [jnp.concatenate(real, axis=1), jnp.concatenate(imag, axis=1)], axis=0
             )
@@ -521,24 +530,23 @@
         settle(recv_f.at[:, pl.ds(0, prompt - 1)], 1)
         maps_ref[...] = dot(synth_ref[...], turn_up(0, 0, cut_at))
         settle(recv_m.at[pl.ds(0, TURNS - 1)], 5)
+        both = recv_m[...].astype(F32).reshape(TURNS * mask_ref.shape[0], LANES)
+        both_t = both.T.astype(BF16)
+        for j in range(TURNS // 2):
+            for at in range(cut):
+                pixmask_ref[j, pl.ds(at * LANES, LANES), :] = dot(both_t, pick_ref[j, at])
         settle(recv_f.at[:, pl.ds(0, n - prompt)], 6)
-        both = recv_m[...].astype(F32).reshape(TURNS * mask_ref.shape[0], LANES)
-        cut = fine // LANES
-        grid = (both.shape[0], LANES)
-        m_turn = div(iota(grid, 1), high_count * sims)
-        m_high = mod(div(iota(grid, 1), sims), high_count)
-        first_row = (m_turn * high_count + m_high) * cut
-        both_t = both.T.astype(BF16)
-        for at in range(cut):
-            pixmask_ref[pl.ds(at * LANES, LANES), :] = dot(
-                both_t, one_hot(iota(grid, 0) == first_row + at)
-            )
         maps = maps_ref[...] + dot(synth_l[...], turn_up(prompt, cut_at, count - cut_at))
-        lead = pixmask_ref[...] * maps[:, :LANES]
         products = jnp.concatenate(
-            [lead * maps[:, LANES : 2 * LANES], lead * maps[:, 2 * LANES :]], axis=1
+            [
+                pixmask_ref[j]
+                * maps[:, 2 * j * LANES : (2 * j + 1) * LANES]
+                * maps[:, (2 * j + 1) * LANES : (2 * j + 2) * LANES]
+                for j in range(TURNS // 2)
+            ],
+            axis=1,
         ).astype(BF16)
-        def bring_down(table, cos_h, sin_h):
+        def bring_down(table, cos_h, sin_h, split):
             size = cos_h.shape[0]
             half = dot(table, products)
             parts = []
@@ -548,9 +556,12 @@
                 parts.append((cos_h * c_part + sin_h * s_part).astype(BF16))
                 parts.append((cos_h * s_part - sin_h * c_part).astype(BF16))
             parts = jnp.concatenate(parts, axis=1)
-            turn = mod(div(iota((8, 4 * LANES), 1), LANES // TURNS), TURNS)[0:1]
+            if not split:
+                return dot(parts, gather_v[:, LANES:]) * pixels ** (-0.5)
+            lane = iota((8, 4 * LANES), 1)
+            turn = (2 * div(lane, 2 * LANES) + mod(div(lane, LANES // 2), 2))[0:1]
             parts = jnp.concatenate([parts * one_hot(turn == t) for t in range(TURNS)], axis=0)
-            return dot(parts, gather_v[...]) * pixels ** (-0.5)
+            return dot(parts, gather_v[:, :LANES]) * pixels ** (-0.5)
 
         def pack(blocks):
             lane_quad = div(iota(blocks[0].shape, 1), 4 * comps)
@@ -563,7 +574,7 @@
             jnp.concatenate([high_ref[part, pl.ds(q * ahead, first)] for q in range(quad)], axis=0)
             for part in range(2)
         ]
-        spectra = bring_down(anal_c[...], *high_c)
+        spectra = bring_down(anal_c[...], *high_c, True)
         for t in range(TURNS):
             at = t * quad * first
             send_p[t, pl.ds(0, 2)] = pack(
@@ -575,22 +586,25 @@
         def _():
             remote(send_p.at[:, 1], recv_p.at[:, seat], 1, 1).start()
 
-        spectra = bring_down(anal_ref[...], high_ref[0], high_ref[1])
+        spectra = bring_down(anal_ref[...], high_ref[0], high_ref[1], False)
         behind = n - prompt
+        rest = [
+            jnp.concatenate(
+                [
+                    spectra[q * ahead + first : (q + 1) * ahead],
+                    spectra[cut_at + q * behind * gh : cut_at + (q + 1) * behind * gh],
+                ],
+                axis=0,
+            )
+            for q in range(quad)
+        ]
         for t in range(TURNS):
-            at = t * count
-            late = at + cut_at
-            rest = [
-                jnp.concatenate(
-                    [
-                        spectra[at + q * ahead + first : at + (q + 1) * ahead],
-                        spectra[late + q * behind * gh : late + (q + 1) * behind * gh],
-                    ],
-                    axis=0,
-                )
-                for q in range(quad)
-            ]
-            send_p[t, pl.ds(2, n - 2)] = pack(rest)
+            send_p[t, pl.ds(2, n - 2)] = pack(
+                [
+                    rest[q] if q == t else pltpu.roll(rest[q], (q - t) * 4 * comps % LANES, 1)
+                    for q in range(quad)
+                ]
+            )
         for d in range(2, n):
             if d % 2 == 0 or d >= 2 * work:
                 remote(send_p.at[:, d], recv_p.at[:, seat], 1, d).start()
@@ -697,15 +711,16 @@
             pltpu.VMEM((total, rows), BF16),
             pltpu.VMEM((total // LANES, LANES, rows), BF16),
             pltpu.VMEM((total // LANES, LANES, rows), BF16),
-            pltpu.VMEM((cycles, 8, LANES), F32),
+            pltpu.VMEM((gh * cycles, LANES), F32),
             pltpu.VMEM((pairs, 2, 8, LANES), F32),
             pltpu.VMEM((fine, 2 * count - count // 2), BF16),
             pltpu.VMEM((fine, count // 2), BF16),
             pltpu.VMEM((2 * count, fine), BF16),
             pltpu.VMEM((count // 4, fine), BF16),
             pltpu.VMEM((2, count, LANES), F32),
-            pltpu.VMEM((fine, LANES), F32),
-            pltpu.VMEM((fine, 3 * LANES), F32),
+            pltpu.VMEM((TURNS // 2, fine, LANES), F32),
+            pltpu.VMEM((fine, 4 * LANES), F32),
+            pltpu.VMEM((TURNS // 2, fine // LANES, TURNS * mask_shape[0], LANES), BF16),
             pltpu.VMEM(mask_shape, BF16),
             pltpu.VMEM((TURNS,) + mask_shape, BF16),
             pltpu.VMEM((TURNS, work, gh, LANES), BF16),

time: 13.1 us -> 13 us (level)
  no operation moved by 1% of the time
where the time goes in v7:
time: 13 us; the launch traced here: 12.9 us
  Pallas kernels  12.2 us (94%)
  between operations  0.64 us (5%)
    pallas_call x1, Pallas kernels, fused(): pl.pallas_call(functools.partial(fused_kernel, n, modes, rows, cycles, pi...  11.6 us
    pallas_call x1, Pallas kernels, fused(): pl.pallas_call(store_kernel, out_shape=(jax.ShapeDtypeStruct(tbar_alm.sha...  0.69 us

profile of v7, /device:TPU:0, one launch (start us, length us, event | category | flops | bytes accessed | tf_op | source)
XLA Modules:
  0.0 12.9 jit_solution(2709163148986937435)
XLA Ops:
  0.6 11.6 %estimator.1 = (f32[8,4,2,257]{3,2,1,0:T(2,128)S(1)}, f32[8,4,2,257]{3,2,1,0:T(2,128)S(1)}) custom-call(s32[128]{0:T(128)} %slots_hbm.1, s32[16]{0:T(128)} %cycle_hbm.1, f32[16]{0:T(128)} %colat_hbm.1, f32[16]{0:T(128)} %weight_hbm.1, s32[1,128]{1,0:T(1,128)} %bitcast.5, bf16[8,4,2,257]{3,2,1,0:T(2,128)(2,1)} %tbar_hbm.1, bf16[8,4,2,257]{3,2,1,0:T(2,128)(2,1)} %twf_hbm.1, ...), custom_call_target="tpu_custom_call" | custom-call | tf_op jit(solution)/shard_map/estimator/pallas_call | solution.py:692
  12.2 0.7 %store.1 = (f32[8,4,2,257]{3,2,1,0:T(2,128)}, f32[8,4,2,257]{3,2,1,0:T(2,128)}) custom-call(f32[8,4,2,257]{3,2,1,0:T(2,128)S(1)} %get-tuple-element.4.grad_ref, f32[8,4,2,257]{3,2,1,0:T(2,128)S(1)} %get-tuple-element.5.curl_ref), custom_call_target="tpu_custom_call" | custom-call | tf_op jit(solution)/shard_map/store/pallas_call | solution.py:739

commit v8 on v7

--- a/solution.py
+++ b/solution.py
@@ -277,17 +277,17 @@
     def slot_of(w, t):
         return 2 * w + t % 2 + t // 2 * 2 * work
 
-    names = [
-        (slots_hbm, slots_s), (colat_hbm, colat_s), (cycle_hbm, cycle_s),
-        (leg_hbm, leg_ref), (tbar_hbm, tbar_ref), (twf_hbm, twf_ref),
-        (mask_hbm, mask_ref), (weight_hbm, weight_s), (row_hbm, slots_v),
-        (mode_hbm, mode_v), (pixel_hbm, pixel_v), (spread_hbm, spread_v), (gather_hbm, gather_v),
+    scalars = [(slots_hbm, slots_s), (colat_hbm, colat_s), (cycle_hbm, cycle_s), (weight_hbm, weight_s)]
+    blocks = [(leg_hbm, leg_ref), (tbar_hbm, tbar_ref), (twf_hbm, twf_ref), (mask_hbm, mask_ref)]
+    tables = [
+        (row_hbm, slots_v), (mode_hbm, mode_v), (pixel_hbm, pixel_v), (spread_hbm, spread_v),
+        (gather_hbm, gather_v),
     ]
-    loads = [
-        pltpu.make_async_copy(source, target, load_sem.at[at])
-        for at, (source, target) in enumerate(names)
+    scalars, blocks, tables = [
+        [pltpu.make_async_copy(source, target, load_sem.at[at]) for source, target in group]
+        for at, group in enumerate((scalars, blocks, tables))
     ]
-    for load in loads[:6]:
+    for load in scalars + blocks:
         load.start()
     barrier = pltpu.get_barrier_semaphore()
 
@@ -299,33 +299,22 @@
                 device_id_type=pl.DeviceIdType.MESH,
             )
 
-    for load in loads[6:8]:
-        load.start()
-
     @pl.when(is_worker)
     def _():
-        for load in loads[8:]:
+        for load in tables:
             load.start()
 
-    def remote(source, target, at, to, mark=None):
+    def remote(source, target, at, to):
         return pltpu.make_async_remote_copy(
-            src_ref=source, dst_ref=target, send_sem=move_sem.at[2 * at],
-            recv_sem=move_sem.at[2 * at + 1 if mark is None else mark], device_id={"ma": to},
+            src_ref=source, dst_ref=target, send_sem=move_sem.at[0],
+            recv_sem=move_sem.at[at], device_id={"ma": to},
             device_id_type=pl.DeviceIdType.MESH,
         )
 
     def settle(buffer, at):
         pltpu.make_async_copy(buffer, buffer, move_sem.at[at]).wait()
 
-    @pl.when(jnp.logical_not(is_worker))
-    def _():
-        pl.semaphore_wait(barrier, work)
-        loads[6].wait()
-        send_m[...] = mask_ref[...].astype(F32).astype(BF16)
-        turn = lax.rem(me, 2) + 2 * lax.div(me, 2 * work)
-        remote(send_m, recv_m.at[turn], 2, 2 * lax.div(lax.rem(me, 2 * work), 2) + 1).start()
-
-    for load in loads[:3]:
+    for load in scalars:
         load.wait()
 
     row_shape = (pairs, rows)
@@ -353,8 +342,16 @@
         for p in range(pairs)
     ]
 
-    for load in loads[3:6]:
+    for load in blocks:
         load.wait()
+
+    @pl.when(jnp.logical_not(is_worker))
+    def _():
+        pl.semaphore_wait(barrier, work)
+        send_m[...] = mask_ref[...].astype(F32).astype(BF16)
+        turn = lax.rem(me, 2) + 2 * lax.div(me, 2 * work)
+        remote(send_m, recv_m.at[turn], 4, 2 * lax.div(lax.rem(me, 2 * work), 2) + 1).start()
+
     lane = iota((8, LANES), 1)
     lane_quad = div(lane, 4 * comps)
     is_phi = mod(div(lane, comps), 4) == 2
@@ -392,13 +389,12 @@
     def _():
         pl.semaphore_wait(barrier, work - 1)
 
-    tardy = 1 + 5 * lax.div(me, prompt)
+    tardy = 1 + lax.div(me, prompt)
     for w in reversed(range(work)):
         @pl.when(me != 2 * w + 1)
         def _():
-            remote(send_f.at[:, w], recv_f.at[:, me], 0, 2 * w + 1, tardy).start()
-
-    loads[7].wait()
+            remote(send_f.at[:, w], recv_f.at[:, me], tardy, 2 * w + 1).start()
+
     lane_shape = (8, LANES)
     keep_lane = iota(lane_shape, 1)
     lane_seat = mod(div(keep_lane, gh), TURNS * work)
@@ -442,7 +438,7 @@
 
     @pl.when(is_worker)
     def _():
-        for load in loads[8:]:
+        for load in tables:
             load.wait()
         pair_count = slots_v.shape[1]
 
@@ -491,7 +487,6 @@
             high_ref[part] = moved[:, at : at + LANES] + moved[:, at + LANES : at + 2 * LANES]
             at += 2 * LANES
 
-        loads[6].wait()
         recv_f[:, me] = send_f[:, seat]
         cut = fine // LANES
         grid = (TURNS * mask_ref.shape[0], LANES)
@@ -529,13 +524,13 @@
 
         settle(recv_f.at[:, pl.ds(0, prompt - 1)], 1)
         maps_ref[...] = dot(synth_ref[...], turn_up(0, 0, cut_at))
-        settle(recv_m.at[pl.ds(0, TURNS - 1)], 5)
+        settle(recv_m.at[pl.ds(0, TURNS - 1)], 4)
         both = recv_m[...].astype(F32).reshape(TURNS * mask_ref.shape[0], LANES)
         both_t = both.T.astype(BF16)
         for j in range(TURNS // 2):
             for at in range(cut):
                 pixmask_ref[j, pl.ds(at * LANES, LANES), :] = dot(both_t, pick_ref[j, at])
-        settle(recv_f.at[:, pl.ds(0, n - prompt)], 6)
+        settle(recv_f.at[:, pl.ds(0, n - prompt)], 2)
         maps = maps_ref[...] + dot(synth_l[...], turn_up(prompt, cut_at, count - cut_at))
         products = jnp.concatenate(
             [
@@ -580,11 +575,11 @@
             send_p[t, pl.ds(0, 2)] = pack(
                 [spectra[at + q * first : at + (q + 1) * first] for q in range(quad)]
             )
-        remote(send_p.at[:, 0], recv_p.at[:, seat], 1, 0).start()
+        remote(send_p.at[:, 0], recv_p.at[:, seat], 3, 0).start()
 
         @pl.when(me != 1)
         def _():
-            remote(send_p.at[:, 1], recv_p.at[:, seat], 1, 1).start()
+            remote(send_p.at[:, 1], recv_p.at[:, seat], 3, 1).start()
 
         spectra = bring_down(anal_ref[...], high_ref[0], high_ref[1], False)
         behind = n - prompt
@@ -607,11 +602,11 @@
             )
         for d in range(2, n):
             if d % 2 == 0 or d >= 2 * work:
-                remote(send_p.at[:, d], recv_p.at[:, seat], 1, d).start()
+                remote(send_p.at[:, d], recv_p.at[:, seat], 3, d).start()
             else:
                 @pl.when(me != d)
                 def _():
-                    remote(send_p.at[:, d], recv_p.at[:, seat], 1, d).start()
+                    remote(send_p.at[:, d], recv_p.at[:, seat], 3, d).start()
         recv_p[:, seat] = send_p[:, me]
         settle(recv_p.at[:, pl.ds(0, work - 1)], 3)
 
@@ -654,18 +649,18 @@
     @pl.when(is_worker)
     def _():
         settle(send_f.at[:, pl.ds(0, work - 1)], 0)
-        settle(send_p.at[:, pl.ds(0, n - 1)], 2)
+        settle(send_p.at[:, pl.ds(0, n - 1)], 0)
 
     @pl.when(jnp.logical_not(is_worker))
     def _():
         settle(send_f, 0)
-        settle(send_m, 4)
+        settle(send_m, 0)
 
 
 def store_kernel(grad_ref, curl_ref, grad_hbm, curl_hbm, sem):
     copies = [
-        pltpu.make_async_copy(grad_ref, grad_hbm, sem.at[0]),
-        pltpu.make_async_copy(curl_ref, curl_hbm, sem.at[1]),
+        pltpu.make_async_copy(grad_ref, grad_hbm, sem),
+        pltpu.make_async_copy(curl_ref, curl_hbm, sem),
     ]
     for copy in copies:
         copy.start()
@@ -727,8 +722,8 @@
             pltpu.VMEM((TURNS, n, gh, LANES), BF16),
             pltpu.VMEM((TURNS, n, gh, LANES), BF16),
             pltpu.VMEM((TURNS, work, gh, LANES), BF16),
-            pltpu.SemaphoreType.DMA((13,)),
-            pltpu.SemaphoreType.DMA((7,)),
+            pltpu.SemaphoreType.DMA((3,)),
+            pltpu.SemaphoreType.DMA((5,)),
         ],
         compiler_params=pltpu.CompilerParams(collective_id=0, has_side_effects=True),
         name="estimator",
@@ -741,7 +736,7 @@
         out_shape=(jax.ShapeDtypeStruct(tbar_alm.shape, F32),) * 2,
         in_specs=[vmem] * 2,
         out_specs=[anywhere] * 2,
-        scratch_shapes=[pltpu.SemaphoreType.DMA((2,))],
+        scratch_shapes=[pltpu.SemaphoreType.DMA],
         name="store",
     )(*(pltpu.with_memory_space_constraint(x, pltpu.VMEM) for x in made))
 

time: 13 us -> 12.9 us (level)
  no operation moved by 1% of the time
where the time goes in v8:
time: 12.9 us; the launch traced here: 12.8 us
  Pallas kernels  12.1 us (94%)
  between operations  0.64 us (5%)
    pallas_call x1, Pallas kernels, fused(): pl.pallas_call(functools.partial(fused_kernel, n, modes, rows, cycles, pi...  11.4 us
    pallas_call x1, Pallas kernels, fused(): pl.pallas_call(store_kernel, out_shape=(jax.ShapeDtypeStruct(tbar_alm.sha...  0.68 us

profile of v8, /device:TPU:0, one launch (start us, length us, event | category | flops | bytes accessed | tf_op | source)
XLA Modules:
  0.0 12.8 jit_solution(13425242615818247118)
XLA Ops:
  0.6 11.4 %estimator.1 = (f32[8,4,2,257]{3,2,1,0:T(2,128)S(1)}, f32[8,4,2,257]{3,2,1,0:T(2,128)S(1)}) custom-call(s32[128]{0:T(128)} %slots_hbm.1, s32[16]{0:T(128)} %cycle_hbm.1, f32[16]{0:T(128)} %colat_hbm.1, f32[16]{0:T(128)} %weight_hbm.1, s32[1,128]{1,0:T(1,128)} %bitcast.5, bf16[8,4,2,257]{3,2,1,0:T(2,128)(2,1)} %tbar_hbm.1, bf16[8,4,2,257]{3,2,1,0:T(2,128)(2,1)} %twf_hbm.1, ...), custom_call_target="tpu_custom_call" | custom-call | tf_op jit(solution)/shard_map/estimator/pallas_call | solution.py:687
  12.1 0.7 %store.1 = (f32[8,4,2,257]{3,2,1,0:T(2,128)}, f32[8,4,2,257]{3,2,1,0:T(2,128)}) custom-call(f32[8,4,2,257]{3,2,1,0:T(2,128)S(1)} %get-tuple-element.4.grad_ref, f32[8,4,2,257]{3,2,1,0:T(2,128)S(1)} %get-tuple-element.5.curl_ref), custom_call_target="tpu_custom_call" | custom-call | tf_op jit(solution)/shard_map/store/pallas_call | solution.py:734

commit v9 on v8

--- a/solution.py
+++ b/solution.py
@@ -253,7 +253,7 @@
     grad_ref, curl_ref,
     slots_s, cycle_s, colat_s, weight_s, slots_v, tbar_ref, twf_ref, leg_ref, mask_ref,
     pixel_v, mode_v, spread_v, gather_v,
-    leg_all, prev_all, leg_p, prev_p, fs_ref, keep_ref, synth_ref, synth_l, anal_ref, anal_c, high_ref,
+    leg_all, prev_all, fold_ref, fs_ref, keep_ref, synth_ref, synth_l, anal_ref, anal_c, high_ref,
     pixmask_ref, maps_ref, pick_ref,
     send_m, recv_m, send_f, recv_f, send_p, recv_p, load_sem, move_sem,
 ):
@@ -285,9 +285,9 @@
     ]
     scalars, blocks, tables = [
         [pltpu.make_async_copy(source, target, load_sem.at[at]) for source, target in group]
-        for at, group in enumerate((scalars, blocks, tables))
+        for at, group in ((0, scalars), (1, blocks), (1, tables))
     ]
-    for load in scalars + blocks:
+    for load in blocks + scalars:
         load.start()
     barrier = pltpu.get_barrier_semaphore()
 
@@ -299,20 +299,17 @@
                 device_id_type=pl.DeviceIdType.MESH,
             )
 
-    @pl.when(is_worker)
-    def _():
-        for load in tables:
-            load.start()
 
     def remote(source, target, at, to):
         return pltpu.make_async_remote_copy(
-            src_ref=source, dst_ref=target, send_sem=move_sem.at[0],
+            src_ref=source, dst_ref=target, send_sem=load_sem.at[0],
             recv_sem=move_sem.at[at], device_id={"ma": to},
             device_id_type=pl.DeviceIdType.MESH,
         )
 
     def settle(buffer, at):
-        pltpu.make_async_copy(buffer, buffer, move_sem.at[at]).wait()
+        sem = load_sem.at[0] if at is None else move_sem.at[at]
+        pltpu.make_async_copy(buffer, buffer, sem).wait()
 
     for load in scalars:
         load.wait()
@@ -345,12 +342,17 @@
     for load in blocks:
         load.wait()
 
+    @pl.when(is_worker)
+    def _():
+        for load in tables:
+            load.start()
+
     @pl.when(jnp.logical_not(is_worker))
     def _():
         pl.semaphore_wait(barrier, work)
         send_m[...] = mask_ref[...].astype(F32).astype(BF16)
         turn = lax.rem(me, 2) + 2 * lax.div(me, 2 * work)
-        remote(send_m, recv_m.at[turn], 4, 2 * lax.div(lax.rem(me, 2 * work), 2) + 1).start()
+        remote(send_m, recv_m.at[turn], 3, 2 * lax.div(lax.rem(me, 2 * work), 2) + 1).start()
 
     lane = iota((8, LANES), 1)
     lane_quad = div(lane, 4 * comps)
@@ -389,7 +391,7 @@
     def _():
         pl.semaphore_wait(barrier, work - 1)
 
-    tardy = 1 + lax.div(me, prompt)
+    tardy = lax.div(me, prompt)
     for w in reversed(range(work)):
         @pl.when(me != 2 * w + 1)
         def _():
@@ -429,12 +431,19 @@
     match = jnp.logical_and(
         row_cycle == mod(place_lane, cycles), mod(place_row, 2) == mod(div(place_lane, cycles), 2)
     )
+    scale = (modes / cycles) ** 0.5 / jnp.sqrt(jnp.maximum(degree * (degree + 1.0), 1.0))
+    kinds = [degree * scale, -(eps * scale), orders * scale]
+    even = mod(div(iota((LANES // 2, rows), 0), 2), groups) == 0
     for k in range(quad // 2):
         place = one_hot(jnp.logical_and(match, row_pair + 2 * k == div(place_lane, span)))
-        leg_p[k] = dot(place, leg_all[...]).astype(BF16)
-        prev_p[k] = dot(place, prev_all[...]).astype(BF16)
-    scale = (modes / cycles) ** 0.5 / jnp.sqrt(jnp.maximum(degree * (degree + 1.0), 1.0))
-    f_level, f_eps, f_order = degree * scale, eps * scale, orders * scale
+        moved_leg = dot(place, leg_all[...])
+        moved_prev = dot(place, prev_all[...])
+        for at, (kind, moved) in enumerate(zip(kinds, (moved_leg, moved_prev, moved_leg))):
+            for side in range(2):
+                p = 2 * k + side
+                factor = jnp.where(even, kind[p : p + 1], kind[quad + p : quad + p + 1])
+                piece = moved[side * LANES // 2 : (side + 1) * LANES // 2] * factor
+                fold_ref[k, pl.ds(at * LANES + side * LANES // 2, LANES // 2), :] = piece.astype(BF16)
 
     @pl.when(is_worker)
     def _():
@@ -522,15 +531,15 @@
                 [jnp.concatenate(real, axis=1), jnp.concatenate(imag, axis=1)], axis=0
             )
 
-        settle(recv_f.at[:, pl.ds(0, prompt - 1)], 1)
+        settle(recv_f.at[:, pl.ds(0, prompt - 1)], 0)
         maps_ref[...] = dot(synth_ref[...], turn_up(0, 0, cut_at))
-        settle(recv_m.at[pl.ds(0, TURNS - 1)], 4)
+        settle(recv_m.at[pl.ds(0, TURNS - 1)], 3)
         both = recv_m[...].astype(F32).reshape(TURNS * mask_ref.shape[0], LANES)
         both_t = both.T.astype(BF16)
         for j in range(TURNS // 2):
             for at in range(cut):
                 pixmask_ref[j, pl.ds(at * LANES, LANES), :] = dot(both_t, pick_ref[j, at])
-        settle(recv_f.at[:, pl.ds(0, n - prompt)], 2)
+        settle(recv_f.at[:, pl.ds(0, n - prompt)], 1)
         maps = maps_ref[...] + dot(synth_l[...], turn_up(prompt, cut_at, count - cut_at))
         products = jnp.concatenate(
             [
@@ -575,11 +584,11 @@
             send_p[t, pl.ds(0, 2)] = pack(
                 [spectra[at + q * first : at + (q + 1) * first] for q in range(quad)]
             )
-        remote(send_p.at[:, 0], recv_p.at[:, seat], 3, 0).start()
+        remote(send_p.at[:, 0], recv_p.at[:, seat], 2, 0).start()
 
         @pl.when(me != 1)
         def _():
-            remote(send_p.at[:, 1], recv_p.at[:, seat], 3, 1).start()
+            remote(send_p.at[:, 1], recv_p.at[:, seat], 2, 1).start()
 
         spectra = bring_down(anal_ref[...], high_ref[0], high_ref[1], False)
         behind = n - prompt
@@ -602,59 +611,50 @@
             )
         for d in range(2, n):
             if d % 2 == 0 or d >= 2 * work:
-                remote(send_p.at[:, d], recv_p.at[:, seat], 3, d).start()
+                remote(send_p.at[:, d], recv_p.at[:, seat], 2, d).start()
             else:
                 @pl.when(me != d)
                 def _():
-                    remote(send_p.at[:, d], recv_p.at[:, seat], 3, d).start()
+                    remote(send_p.at[:, d], recv_p.at[:, seat], 2, d).start()
         recv_p[:, seat] = send_p[:, me]
-        settle(recv_p.at[:, pl.ds(0, work - 1)], 3)
+        settle(recv_p.at[:, pl.ds(0, work - 1)], 2)
 
     @pl.when(jnp.logical_not(is_worker))
     def _():
-        settle(recv_p, 3)
+        settle(recv_p, 2)
 
     came = recv_p[...].astype(F32).reshape(TURNS * work * gh, LANES)
     came = jnp.concatenate([came, came], axis=0).T
-    here, before = {}, {}
+    made = {}
     for k in range(quad // 2):
         members = [p for p in range(pairs) if p % quad // 2 == k]
-        first_k, second_k = [], []
+        columns = [[], [], []]
         for p in members:
             at = p % quad * 4 * comps
             four = [came[at + g * comps : at + (g + 1) * comps] for g in range(4)]
             with_cos, with_sin = keep_ref[p, 0], keep_ref[p, 1]
-            first_k += [four[0] * with_cos, four[1] * with_cos]
-            first_k += [four[2] * with_sin, four[3] * with_sin]
-            second_k += [four[0] * with_sin, four[1] * with_sin]
-        out_a = dot(jnp.concatenate(first_k, axis=0).astype(BF16), leg_p[k])
-        out_b = dot(jnp.concatenate(second_k, axis=0).astype(BF16), prev_p[k])
+            columns[0] += [four[0] * with_cos, four[1] * with_cos]
+            columns[1] += [four[0] * with_sin, four[1] * with_sin]
+            columns[2] += [four[2] * with_sin, four[3] * with_sin]
+        stacked = [jnp.concatenate(column, axis=0).astype(BF16) for column in columns]
+        out = dot(jnp.concatenate(stacked, axis=1), fold_ref[k])
         for at, p in enumerate(members):
-            here[p] = out_a[at * 4 * comps : (at + 1) * 4 * comps]
-            before[p] = out_b[at * 2 * comps : (at + 1) * 2 * comps]
+            made[p] = out[at * 2 * comps : (at + 1) * 2 * comps]
     for p in range(pairs):
-        lev, ep, az = f_level[p : p + 1], f_eps[p : p + 1], f_order[p : p + 1]
-        grad = (
-            lev * here[p][:comps] - ep * before[p][:comps]
-            + az * here[p][2 * comps : 3 * comps]
-        )
-        curl = (
-            lev * here[p][comps : 2 * comps] - ep * before[p][comps:]
-            + az * here[p][3 * comps :]
-        )
+        grad, curl = made[p][:comps], made[p][comps:]
         for s in range(sims):
             grad_ref[p, s] = grad[2 * s : 2 * s + 2]
             curl_ref[p, s] = curl[2 * s : 2 * s + 2]
 
     @pl.when(is_worker)
     def _():
-        settle(send_f.at[:, pl.ds(0, work - 1)], 0)
-        settle(send_p.at[:, pl.ds(0, n - 1)], 0)
+        settle(send_f.at[:, pl.ds(0, work - 1)], None)
+        settle(send_p.at[:, pl.ds(0, n - 1)], None)
 
     @pl.when(jnp.logical_not(is_worker))
     def _():
-        settle(send_f, 0)
-        settle(send_m, 0)
+        settle(send_f, None)
+        settle(send_m, None)
 
 
 def store_kernel(grad_ref, curl_ref, grad_hbm, curl_hbm, sem):
@@ -704,8 +704,7 @@
         + [
             pltpu.VMEM((total, rows), BF16),
             pltpu.VMEM((total, rows), BF16),
-            pltpu.VMEM((total // LANES, LANES, rows), BF16),
-            pltpu.VMEM((total // LANES, LANES, rows), BF16),
+            pltpu.VMEM((total // LANES, 3 * LANES, rows), BF16),
             pltpu.VMEM((gh * cycles, LANES), F32),
             pltpu.VMEM((pairs, 2, 8, LANES), F32),
             pltpu.VMEM((fine, 2 * count - count // 2), BF16),
@@ -722,8 +721,8 @@
             pltpu.VMEM((TURNS, n, gh, LANES), BF16),
             pltpu.VMEM((TURNS, n, gh, LANES), BF16),
             pltpu.VMEM((TURNS, work, gh, LANES), BF16),
-            pltpu.SemaphoreType.DMA((3,)),
-            pltpu.SemaphoreType.DMA((5,)),
+            pltpu.SemaphoreType.DMA((2,)),
+            pltpu.SemaphoreType.DMA((4,)),
         ],
         compiler_params=pltpu.CompilerParams(collective_id=0, has_side_effects=True),
         name="estimator",

time: 12.9 us -> 12.9 us (level)
  no operation moved by 1% of the time
where the time goes in v9:
time: 12.9 us; the launch traced here: 12.7 us
  Pallas kernels  12.1 us (94%)
  between operations  0.64 us (5%)
    pallas_call x1, Pallas kernels, fused(): pl.pallas_call(functools.partial(fused_kernel, n, modes, rows, cycles, pi...  11.4 us
    pallas_call x1, Pallas kernels, fused(): pl.pallas_call(store_kernel, out_shape=(jax.ShapeDtypeStruct(tbar_alm.sha...  0.68 us

profile of v9, /device:TPU:0, one launch (start us, length us, event | category | flops | bytes accessed | tf_op | source)
XLA Modules:
  0.0 12.7 jit_solution(3705295453399863905)
XLA Ops:
  0.6 11.4 %estimator.1 = (f32[8,4,2,257]{3,2,1,0:T(2,128)S(1)}, f32[8,4,2,257]{3,2,1,0:T(2,128)S(1)}) custom-call(s32[128]{0:T(128)} %slots_hbm.1, s32[16]{0:T(128)} %cycle_hbm.1, f32[16]{0:T(128)} %colat_hbm.1, f32[16]{0:T(128)} %weight_hbm.1, s32[1,128]{1,0:T(1,128)} %bitcast.5, bf16[8,4,2,257]{3,2,1,0:T(2,128)(2,1)} %tbar_hbm.1, bf16[8,4,2,257]{3,2,1,0:T(2,128)(2,1)} %twf_hbm.1, ...), custom_call_target="tpu_custom_call" | custom-call | tf_op jit(solution)/shard_map/estimator/pallas_call | solution.py:687
  12.0 0.7 %store.1 = (f32[8,4,2,257]{3,2,1,0:T(2,128)}, f32[8,4,2,257]{3,2,1,0:T(2,128)}) custom-call(f32[8,4,2,257]{3,2,1,0:T(2,128)S(1)} %get-tuple-element.4.grad_ref, f32[8,4,2,257]{3,2,1,0:T(2,128)S(1)} %get-tuple-element.5.curl_ref), custom_call_target="tpu_custom_call" | custom-call | tf_op jit(solution)/shard_map/store/pallas_call | solution.py:733

commit v10 on v9

--- a/solution.py
+++ b/solution.py
@@ -621,6 +621,8 @@
 
     @pl.when(jnp.logical_not(is_worker))
     def _():
+        settle(send_f, None)
+        settle(send_m, None)
         settle(recv_p, 2)
 
     came = recv_p[...].astype(F32).reshape(TURNS * work * gh, LANES)
@@ -650,11 +652,6 @@
     def _():
         settle(send_f.at[:, pl.ds(0, work - 1)], None)
         settle(send_p.at[:, pl.ds(0, n - 1)], None)
-
-    @pl.when(jnp.logical_not(is_worker))
-    def _():
-        settle(send_f, None)
-        settle(send_m, None)
 
 
 def store_kernel(grad_ref, curl_ref, grad_hbm, curl_hbm, sem):

time: 12.9 us -> 12.9 us (level)
  no operation moved by 1% of the time
where the time goes in v10:
time: 12.9 us; the launch traced here: 12.7 us
  Pallas kernels  12.1 us (94%)
  between operations  0.64 us (5%)
    pallas_call x1, Pallas kernels, fused(): pl.pallas_call(functools.partial(fused_kernel, n, modes, rows, cycles, pi...  11.4 us
    pallas_call x1, Pallas kernels, fused(): pl.pallas_call(store_kernel, out_shape=(jax.ShapeDtypeStruct(tbar_alm.sha...  0.68 us

profile of v10, /device:TPU:0, one launch (start us, length us, event | category | flops | bytes accessed | tf_op | source)
XLA Modules:
  0.0 12.7 jit_solution(1513705922782965920)
XLA Ops:
  0.6 11.4 %estimator.1 = (f32[8,4,2,257]{3,2,1,0:T(2,128)S(1)}, f32[8,4,2,257]{3,2,1,0:T(2,128)S(1)}) custom-call(s32[128]{0:T(128)} %slots_hbm.1, s32[16]{0:T(128)} %cycle_hbm.1, f32[16]{0:T(128)} %colat_hbm.1, f32[16]{0:T(128)} %weight_hbm.1, s32[1,128]{1,0:T(1,128)} %bitcast.5, bf16[8,4,2,257]{3,2,1,0:T(2,128)(2,1)} %tbar_hbm.1, bf16[8,4,2,257]{3,2,1,0:T(2,128)(2,1)} %twf_hbm.1, ...), custom_call_target="tpu_custom_call" | custom-call | tf_op jit(solution)/shard_map/estimator/pallas_call | solution.py:684
  12.0 0.7 %store.1 = (f32[8,4,2,257]{3,2,1,0:T(2,128)}, f32[8,4,2,257]{3,2,1,0:T(2,128)}) custom-call(f32[8,4,2,257]{3,2,1,0:T(2,128)S(1)} %get-tuple-element.4.grad_ref, f32[8,4,2,257]{3,2,1,0:T(2,128)S(1)} %get-tuple-element.5.curl_ref), custom_call_target="tpu_custom_call" | custom-call | tf_op jit(solution)/shard_map/store/pallas_call | solution.py:730
